TPU v7x, 32 devices: a whole 2x2x4 slice. The times are simulated.
32 devices in a mesh: rep: 1, dp: 32 (over x, y, z, core).
Axes of the slice: x: 2, y: 2, z: 4, core: 2. Of those that a mesh axis runs over, the one named last changes fastest.
Arguments:
- x: bfloat16 [32, 2048, 640], P(('rep', 'dp'))
- dy: bfloat16 [32, 2048, 640], P(('rep', 'dp'))
- w_gate: bfloat16 [2, 640, 2560], P(None, 'dp')
- w_up: bfloat16 [2, 640, 2560], P(None, 'dp')
- w_down: bfloat16 [2, 2560, 640], P(None, 'dp')
Outputs:
- output 1: bfloat16 [32, 2048, 640], P(('rep', 'dp'))
- output 2: bfloat16 [2, 640, 2560], P('rep', 'dp')
- output 3: bfloat16 [2, 640, 2560], P('rep', 'dp')
- output 4: bfloat16 [2, 2560, 640], P('rep', 'dp')
All inputs are finite; a program needn't handle non-finite values.
Results may differ from a plain program's by a relative error of at most 0.018.
Values are sent between devices in bfloat16 or wider.
A program may use at most 2 GiB of HBM per device.

v0:
```python
import jax
import jax.numpy as jnp
from jax import lax

NAMES = ("w_gate", "w_up", "w_down")


def matmul(a, w):
    return jnp.dot(a, w, preferred_element_type=jnp.float32).astype(jnp.bfloat16)


def normed(h):
    wide = h.astype(jnp.float32)
    scale = lax.rsqrt(jnp.mean(wide**2, -1, keepdims=True) + 1e-6)
    return (wide * scale).astype(jnp.bfloat16)


def layer(h, w):
    a = normed(h)
    gate = jnp.dot(a, w["w_gate"], preferred_element_type=jnp.float32)
    up = jnp.dot(a, w["w_up"], preferred_element_type=jnp.float32)
    return h + matmul((jax.nn.silu(gate) * up).astype(jnp.bfloat16), w["w_down"])


def stack(weights, h):
    for number in range(weights["w_gate"].shape[0]):
        h = layer(h, {name: w[number] for name, w in weights.items()})
    return h


def solution(mesh):
    groups = mesh.shape["rep"]

    def step(x, dy, *weights):
        shape = x.shape
        x, dy = (t.reshape(groups, -1, *t.shape[1:]) for t in (x, dy))

        def of_a_group(x, dy):
            _, back = jax.vjp(stack, dict(zip(NAMES, weights, strict=True)), x)
            by_weights, by_x = back(dy)
            return (by_x, *(by_weights[name] for name in NAMES))

        by_x, *by_weights = jax.vmap(of_a_group)(x, dy)
        return (by_x.reshape(shape), *(t.reshape(-1, *t.shape[2:]) for t in by_weights))

    return step
```

profile of v0, /device:TPU:0, one launch (start us, length us, event | category | flops | bytes accessed | tf_op | source)
XLA Modules:
  0.0 1843.7 jit_solution(2747653298864692126)
XLA Ops:
  33.5 176.3 %while.13 = (bf16[1,2048,640]{2,1,0:T(8,128)(2,1)S(1)}, bf16[1,80,640]{2,1,0:T(8,128)(2,1)S(1)}, bf16[1,2048,2560]{1,2,0:T(8,128)(2,1)}, bf16[1,80,640]{2,1,0:T(...) while((bf16[1,2048,640]{2,1,0:T(8,128)(2,1)S(1)}, ...), condition=%wide.windowed_dot_general_cond_ag, body=%wide.windowed_dot_general_body_ag.sunk | while | flops 839065600 | bytes 11223581 | solution.py:9
  33.5 6.4 collective-permute-start
  209.8 13.8 copy.24
  223.7 15.8 fusion.202
  239.4 26.6 %fusion.176 = (bf16[1,2048,2560]{2,1,0:T(8,128)(2,1)}, f32[2048,2560]{1,0:T(8,128)}) fusion(f32[2048,2560]{1,0:T(8,128)} %fusion.202, bf16[1,640,2560]{2,0,1:T(2,128)(2,1)} %all-gather.29.cloned.1.call-done, bf16[1,2048,640]{1,2,0:T(8,128)(2,1)} %fusion.187), kind=kOutput, calls=%fused_computation.215 | convolution fusion | flops 6742343680 | bytes 58327040 | tf_op jit(solution)/vmap(jvp())/dot_general | solution.py:21
  266.0 14.5 copy.28
  280.5 11.4 fusion.189
  297.5 16.0 fusion.196
  313.5 56.4 %all-gather.35.cloned.1.call-done = bf16[1,640,2560]{2,0,1:T(2,128)(2,1)} async-done(((bf16[1,20,2560]{2,0,1:T(2,128)(2,1)}), bf16[1,640,2560]{2,0,1:T(2,128)(2,1)}) %all-gather.35.cloned.1.call-update) | async-done | bytes 3276816 | tf_op jit(solution)/vmap(jvp())/squeeze | solution.py:27
  369.9 26.1 %fusion.170 = (bf16[1,2048,2560]{2,1,0:T(8,128)(2,1)}, f32[2048,2560]{1,0:T(8,128)}) fusion(f32[2048,2560]{1,0:T(8,128)} %fusion.196, bf16[1,640,2560]{2,0,1:T(2,128)(2,1)} %all-gather.35.cloned.1.call-done, bf16[1,2048,640]{1,2,0:T(8,128)(2,1)} %fusion.190), kind=kOutput, calls=%fused_computation.205 | convolution fusion | flops 6742343680 | bytes 58327040 | tf_op jit(solution)/vmap(jvp())/dot_general | solution.py:21
  396.0 14.6 copy.26
  410.6 178.2 %while.18 = (bf16[1,2048,2560]{1,2,0:T(8,128)(2,1)}, bf16[1,2048,640]{2,1,0:T(8,128)(2,1)S(1)}, f32[80,640]{1,0:T(8,128)S(1)}, f32[80,640]{1,0:T(8,128)}, u32[]{...) while((bf16[1,2048,2560]{1,2,0:T(8,128)(2,1)}, ...), condition=%wide.windowed_dot_general_cond_rs.4.clone, body=%wide.windowed_dot_general_body_rs.4.clone.sunk | while | flops 841789440 | bytes 75530856 | solution.py:9
  589.5 19.4 %fusion.161 = (bf16[1,2048,2560]{2,1,0:T(8,128)(2,1)S(1)}, bf16[1,2048,2560]{2,1,0:T(8,128)(2,1)S(1)}) fusion(f32[2048,2560]{1,0:T(8,128)} %fusion.196, f32[2048,2560]{1,0:T(8,128)} %get-tuple-element.318, bf16[1,2048,2560]{2,1,0:T(8,128)(2,1)} %copy.24), kind=kLoop, calls=%fused_computation.195 | loop fusion | flops 78643200 | bytes 73400320 | tf_op jit(solution)/vmap(transpose(jvp(jit(silu))))/add_any | solution.py:22
  608.9 13.4 fusion.211
  622.3 12.3 fusion.191
  641.3 187.5 %while.19 = (bf16[1,2048,640]{2,1,0:T(8,128)(2,1)}, bf16[1,2048,2560]{1,2,0:T(8,128)(2,1)}, f32[640,80]{0,1:T(8,128)S(1)}, f32[640,80]{0,1:T(8,128)}, u32[]{:T(1...) while((bf16[1,2048,640]{2,1,0:T(8,128)(2,1)}, ...), condition=%wide.windowed_dot_general_cond_rs.5.clone, body=%wide.windowed_dot_general_body_rs.5.clone.sunk | while | flops 841789440 | bytes 75530856 | solution.py:9
  829.5 231.0 %while.16 = (bf16[1,2048,2560]{2,1,0:T(8,128)(2,1)}, bf16[1,2048,640]{1,2,0:T(8,128)(2,1)S(1)}, f32[2560,20]{0,1:T(8,128)S(1)}, f32[2560,20]{0,1:T(8,128)}, u32[...) while((bf16[1,2048,2560]{2,1,0:T(8,128)(2,1)}, ...), condition=%wide.windowed_dot_general_cond_rs.2.clone, body=%wide.windowed_dot_general_body_rs.2.clone.sunk | while | flops 839823360 | bytes 34407020 | solution.py:21
  836.3 5.8 fusion.363
  849.3 5.8 fusion.365
  878.3 5.8 fusion.365
  907.3 5.8 fusion.365
  936.3 5.8 fusion.365
  965.3 5.8 fusion.365
  994.3 5.8 fusion.365
  1023.2 5.8 fusion.365
  1052.2 5.8 fusion.365
  1061.3 29.2 %fusion.163 = (bf16[1,2048,2560]{2,1,0:T(8,128)(2,1)}, bf16[1,2048,2560]{2,1,0:T(8,128)(2,1)}) fusion(f32[2048,2560]{1,0:T(8,128)} %fusion.202, f32[2048,2560]{1,0:T(8,128)} %get-tuple-element.310, bf16[1,2560,640]{2,1,0:T(8,128)(2,1)} %all-gather.31.cloned.1.call-done, bf16[1,2048,640]{1,2,0:T(8,128)(2,1)} %copy-done.8), kind=kOutput, calls=%fused_computation.197 | convolution fusion | flops 6794772480 | bytes 68812800 | tf_op jit(solution)/vmap(transpose(jvp()))/dot_general | solution.py:9
  1090.4 231.4 %while.17 = (bf16[1,2048,2560]{2,1,0:T(8,128)(2,1)}, bf16[1,2048,640]{1,2,0:T(8,128)(2,1)S(1)}, f32[2560,20]{0,1:T(8,128)S(1)}, f32[2560,20]{0,1:T(8,128)}, u32[...) while((bf16[1,2048,2560]{2,1,0:T(8,128)(2,1)}, ...), condition=%wide.windowed_dot_general_cond_rs.3.clone, body=%wide.windowed_dot_general_body_rs.3.clone.sunk | while | flops 839823360 | bytes 34407020 | solution.py:21
  1155.3 5.8 fusion.371
  1168.3 5.8 fusion.373
  1242.4 5.8 fusion.371
  1255.4 5.8 fusion.373
  1322.5 236.8 %while.14 = (bf16[1,2048,2560]{2,1,0:T(8,128)(2,1)}, bf16[1,2048,640]{1,2,0:T(8,128)(2,1)}, f32[2560,20]{0,1:T(8,128)}, f32[2560,20]{0,1:T(8,128)}, u32[]{:T(128...) while((bf16[1,2048,2560]{2,1,0:T(8,128)(2,1)}, ...), condition=%wide.windowed_dot_general_cond_rs.clone, body=%wide.windowed_dot_general_body_rs.clone.sunk | while | flops 839823360 | bytes 33587792 | solution.py:20
  1329.3 6.0 fusion.347
  1342.6 6.0 fusion.349
  1359.1 6.0 fusion.347
  1372.4 6.0 fusion.349
  1389.0 6.0 fusion.347
  1402.2 6.0 fusion.349
  1418.8 6.0 fusion.347
  1432.1 6.0 fusion.349
  1448.6 6.0 fusion.347
  1461.9 6.0 fusion.349
  1478.5 6.0 fusion.347
  1491.7 6.0 fusion.349
  1508.3 6.0 fusion.347
  1521.6 6.0 fusion.349
  1538.1 5.9 fusion.347
  1551.4 6.0 fusion.349
  1559.3 231.8 %while.15 = (bf16[1,2048,2560]{2,1,0:T(8,128)(2,1)}, bf16[1,2048,640]{1,2,0:T(8,128)(2,1)S(1)}, f32[2560,20]{0,1:T(8,128)S(1)}, f32[2560,20]{0,1:T(8,128)}, u32[...) while((bf16[1,2048,2560]{2,1,0:T(8,128)(2,1)}, ...), condition=%wide.windowed_dot_general_cond_rs.1.clone, body=%wide.windowed_dot_general_body_rs.1.clone.sunk | while | flops 839823360 | bytes 34407020 | solution.py:20
  1579.3 5.8 fusion.357
  1595.3 5.8 fusion.355
  1608.3 5.8 fusion.357
  1624.4 5.8 fusion.355
  1637.4 5.8 fusion.357
  1666.5 5.8 fusion.357
  1695.5 5.8 fusion.357
  1711.6 5.8 fusion.355
  1724.6 5.8 fusion.357
  1753.6 5.8 fusion.357
  1782.7 5.8 fusion.357
  1791.1 11.8 fusion.221
  1803.0 11.4 fusion.188
  1822.7 7.7 collective-permute-done.29
  (959 shorter events, 1284.6 us)
Async XLA Ops:
  7.2 216.5 %all-gather.27.cloned.1.call-start = ((), (), s32[]{:S(2)}) async-start(), calls=%async_computation | async-start | bytes 6758400 | tf_op jit(solution)/vmap(jvp())/squeeze | solution.py:27
  9.4 230.1 %all-gather.29.cloned.1.call-start = ((), (), s32[]{:S(2)}) async-start(), calls=%async_computation.1 | async-start | bytes 6758400 | tf_op jit(solution)/vmap(jvp())/squeeze | solution.py:27
  11.6 269.0 %all-gather.31.cloned.1.call-start = ((), (), s32[]{:S(2)}) async-start(), calls=%async_computation.2 | async-start | bytes 3379200 | tf_op jit(solution)/vmap(jvp())/squeeze | solution.py:27
  13.3 284.3 %all-gather.33.cloned.1.call-start = ((), (), s32[]{:S(2)}) async-start(), calls=%async_computation.3 | async-start | bytes 6758400 | tf_op jit(solution)/vmap(jvp())/squeeze | solution.py:27
  13.8 356.1 %all-gather.35.cloned.1.call-start = ((), (), s32[]{:S(2)}) async-start(), calls=%async_computation.4 | async-start | bytes 6758400 | tf_op jit(solution)/vmap(jvp())/squeeze | solution.py:27
  13.9 14.4 collective-permute-start.28
  588.8 1245.2 %collective-permute-start.33 = (f32[80,640]{1,0:T(8,128)}, f32[80,640]{1,0:T(8,128)}, u32[]{:S(2)}, u32[]{:S(2)}) collective-permute-start(f32[80,640]{1,0:T(8,128)} %get-tuple-element.52), channel_id=46, source_target_pairs={{0,1},{1,2},{2,3},{3,4},{4,5},{5,6},{6,7},{7,8},{8,9},{9,10},{10,1... | collective-permute-start | bytes 614408 | tf_op jit(solution)/vmap(transpose(jvp()))/dot_general | solution.py:9
  828.9 1006.1 %collective-permute-start.34 = (f32[640,80]{0,1:T(8,128)}, f32[640,80]{0,1:T(8,128)}, u32[]{:S(2)}, u32[]{:S(2)}) collective-permute-start(f32[640,80]{0,1:T(8,128)} %get-tuple-element.54), channel_id=52, source_target_pairs={{0,1},{1,2},{2,3},{3,4},{4,5},{5,6},{6,7},{7,8},{8,9},{9,10},{10,1... | collective-permute-start | bytes 614408 | tf_op jit(solution)/vmap(transpose(jvp()))/dot_general | solution.py:9
  830.2 11.9 collective-permute-start.12
  843.9 11.9 collective-permute-start.15
  859.3 11.9 collective-permute-start.12
  872.9 11.9 collective-permute-start.15
  888.3 11.9 collective-permute-start.12
  901.9 11.9 collective-permute-start.15
  917.3 11.9 collective-permute-start.12
  930.9 11.9 collective-permute-start.15
  946.2 11.9 collective-permute-start.12
  959.9 11.9 collective-permute-start.15
  975.2 11.9 collective-permute-start.12
  988.9 11.9 collective-permute-start.15
  1004.2 11.9 collective-permute-start.12
  1017.9 11.9 collective-permute-start.15
  1033.2 11.9 collective-permute-start.12
  1046.9 11.9 collective-permute-start.15
  1060.6 760.0 %collective-permute-start.31 = (f32[2560,20]{0,1:T(8,128)}, f32[2560,20]{0,1:T(8,128)}, u32[]{:S(2)}, u32[]{:S(2)}) collective-permute-start(f32[2560,20]{0,1:T(8,128)} %get-tuple-element.48), channel_id=34, source_target_pairs={{0,1},{1,2},{2,3},{3,4},{4,5},{5,6},{6,7},{7,8},{8,9},{9,10},{10,1... | collective-permute-start | bytes 614408 | tf_op jit(solution)/vmap(transpose(jvp()))/dot_general | solution.py:21
  1091.2 11.9 collective-permute-start.16
  1120.2 11.9 collective-permute-start.16
  1133.9 11.9 collective-permute-start.19
  1149.2 11.9 collective-permute-start.16
  1162.9 11.9 collective-permute-start.19
  1178.3 11.9 collective-permute-start.16
  1207.3 11.9 collective-permute-start.16
  1221.0 11.9 collective-permute-start.19
  1236.4 11.9 collective-permute-start.16
  1250.1 11.9 collective-permute-start.19
  1265.4 11.9 collective-permute-start.16
  1294.4 11.9 collective-permute-start.16
  1308.1 11.9 collective-permute-start.19
  1323.2 12.1 collective-permute-start.4
  1352.1 13.0 collective-permute-start.4
  1382.0 13.0 collective-permute-start.4
  1411.8 13.0 collective-permute-start.4
  1441.6 13.0 collective-permute-start.4
  1471.5 13.0 collective-permute-start.4
  1501.3 13.0 collective-permute-start.4
  1531.1 13.0 collective-permute-start.4
  1560.2 11.9 collective-permute-start.8
  1573.9 11.9 collective-permute-start.11
  1589.3 11.9 collective-permute-start.8
  1603.0 11.9 collective-permute-start.11
  1618.3 11.9 collective-permute-start.8
  1632.1 11.9 collective-permute-start.11
  1647.4 11.9 collective-permute-start.8
  1661.1 11.9 collective-permute-start.11
  1676.4 11.9 collective-permute-start.8
  1690.2 11.9 collective-permute-start.11
  1705.5 11.9 collective-permute-start.8
  1719.2 11.9 collective-permute-start.11
  1734.6 11.9 collective-permute-start.8
  1748.3 11.9 collective-permute-start.11
  1763.6 11.9 collective-permute-start.8
  1777.4 11.9 collective-permute-start.11
  1791.0 30.6 %collective-permute-start.32 = (f32[2560,20]{0,1:T(8,128)}, f32[2560,20]{0,1:T(8,128)}, u32[]{:S(2)}, u32[]{:S(2)}) collective-permute-start(f32[2560,20]{0,1:T(8,128)} %get-tuple-element.50), channel_id=40, source_target_pairs={{0,1},{1,2},{2,3},{3,4},{4,5},{5,6},{6,7},{7,8},{8,9},{9,10},{10,1... | collective-permute-start | bytes 614408 | tf_op jit(solution)/vmap(transpose(jvp()))/dot_general | solution.py:21
  1820.6 12.5 collective-permute-start.30
  (245 other events, 2800.3 us)
Sparse Core Ops, SparseCore 0:
  11.4 76.1 all-gather.26
  90.4 73.8 all-gather.28
  167.1 58.2 all-gather.30
  228.7 68.7 all-gather.32
  300.8 69.0 all-gather.34
where the time goes:
time: 1860 us; the launch traced here: 1840 us
  matrix products  640 us (34%)
  starting transfers between devices  534 us (29%)
  other arithmetic  274 us (15%)
  waiting for transfers between devices  265 us (14%)
  local copies, waits for them, and re-layouts  114 us (6%)
    dot_general x36, matrix products, layer(): up = jnp.dot(a, w['w_up'], preferred_element_type=jnp.float32)  263 us
    dot_general x36, matrix products, layer(): gate = jnp.dot(a, w['w_gate'], preferred_element_type=jnp.float32)  244 us
    dot_general x99, waiting for transfers between devices, matmul(): jnp.dot(a, w, preferred_element_type=jnp.float32).astype(jnp.bfloat16)  196 us
    dot_general x99, starting transfers between devices, matmul(): jnp.dot(a, w, preferred_element_type=jnp.float32).astype(jnp.bfloat16)  192 us
    dot_general x66, starting transfers between devices, layer(): up = jnp.dot(a, w['w_up'], preferred_element_type=jnp.float32)  171 us
    dot_general x66, starting transfers between devices, layer(): gate = jnp.dot(a, w['w_gate'], preferred_element_type=jnp.float32)  171 us
    dot_general x50, matrix products, matmul(): jnp.dot(a, w, preferred_element_type=jnp.float32).astype(jnp.bfloat16)  133 us
    dot_general x96, other arithmetic  104 us
  transfers between devices with their start and end apart: 236, of which 65 were waited for; matrix products, arithmetic and copies ran while one was open for 51% of the time, Pallas kernels for 0%

commit v1 on v0

v1 whole, which is shorter than its diff:
```python
import jax
import jax.numpy as jnp
from jax import lax
from jax.sharding import PartitionSpec as P

LAYERS = 2
BF = jnp.bfloat16
F32 = jnp.float32


def dot(a, b, dims):
    return lax.dot_general(a, b, (dims, ((), ())), preferred_element_type=F32)


NN = ((1,), (0,))
NT = ((1,), (1,))
TN = ((0,), (0,))


GROUP = 4


def exchange(t):
    n = lax.axis_size("dp")
    groups = [[g + i for i in range(GROUP)] for g in range(0, n, GROUP)]
    return lax.all_to_all(t, "dp", 0, 0, axis_index_groups=groups, tiled=True)


def gather(w):
    return lax.all_gather(w, "dp", axis=0, tiled=True)


def scatter(g):
    return lax.psum_scatter(g, "dp", scatter_dimension=0, tiled=True)


def rows_to_blocks(w):
    m, r, f = w.shape
    t = w.reshape(m, r, GROUP, f // GROUP).transpose(2, 0, 1, 3)
    t = exchange(t)
    return t.transpose(1, 0, 2, 3).reshape(m, GROUP * r, f // GROUP)


def blocks_to_rows(b):
    m, r, f = b.shape
    t = b.reshape(m, GROUP, r // GROUP, f).transpose(1, 0, 2, 3)
    t = exchange(t)
    return t.transpose(1, 2, 0, 3).reshape(m, r // GROUP, GROUP * f)


def whole(blocks):
    t = blocks.reshape(-1, GROUP, 80, 640).transpose(0, 2, 1, 3)
    return t.reshape(640, 2560)


def apart(g):
    t = g.reshape(-1, 80, GROUP, 640).transpose(0, 2, 1, 3)
    return t.reshape(-1, 640)


def step(x, dy, wg, wu, wd):
    h = x[0]
    ct = dy[0]
    mine = rows_to_blocks(jnp.concatenate([wg, wu]))
    wgs = [whole(gather(mine[l])) for l in range(LAYERS)]
    wus = [whole(gather(mine[LAYERS + l])) for l in range(LAYERS)]
    wds = [gather(wd[l]) for l in range(LAYERS)]
    saved = []
    for l in range(LAYERS):
        wide = h.astype(F32)
        scale = lax.rsqrt(jnp.mean(wide**2, -1, keepdims=True) + 1e-6)
        a = (wide * scale).astype(BF)
        g = dot(a, wgs[l], NN)
        u = dot(a, wus[l], NN)
        act = (jax.nn.silu(g) * u).astype(BF)
        saved.append((h, scale, a, g, u, act))
        if l < LAYERS - 1:
            h = h + dot(act, wds[l], NN).astype(BF)
    outs = [None] * LAYERS
    for l in reversed(range(LAYERS)):
        h, scale, a, g, u, act = saved[l]
        dact = dot(ct, wds[l], NT).astype(BF).astype(F32)
        s = jax.nn.sigmoid(g)
        du = (dact * (g * s)).astype(BF)
        dg = (dact * u * (s * (1 + g * (1 - s)))).astype(BF)
        dwd = dot(act, ct, TN).astype(BF)
        dwg = dot(a, dg, TN).astype(BF)
        dwu = dot(a, du, TN).astype(BF)
        outs[l] = (scatter(apart(dwg)), scatter(apart(dwu)), scatter(dwd))
        da = (dot(dg, wgs[l], NT) + dot(du, wus[l], NT)).astype(BF).astype(F32)
        wide = h.astype(F32)
        inner = jnp.mean(da * wide, -1, keepdims=True)
        dh = da * scale - wide * (scale * scale * scale * inner)
        ct = ct + dh.astype(BF)
    back = blocks_to_rows(jnp.stack([outs[l][i] for i in range(2) for l in range(LAYERS)]))
    return ct[None], back[:LAYERS], back[LAYERS:], jnp.stack([outs[l][2] for l in range(LAYERS)])


def solution(mesh):
    w = P(None, "dp", None)
    t = P(("rep", "dp"), None, None)
    o = P("rep", "dp", None)
    return jax.shard_map(step, mesh=mesh, in_specs=(t, t, w, w, w), out_specs=(t, o, o, o), check_vma=False)
```

time: 1860 us -> 1290 us (0.69)
  waiting for transfers between devices: 265 us -> 916 us
  starting transfers between devices: 534 us -> 4.73 us
  matrix products: 640 us -> 240 us
  other arithmetic: 274 us -> 14.1 us
  local copies, waits for them, and re-layouts: 114 us -> 85.9 us
    reduce_scatter x0 -> x6, waiting for transfers between devices: none -> 646 us  [scatter(): return lax.psum_scatter(g, 'dp', scatter_dimension=0, tiled=True)]
    dot_general x231 -> x0, starting transfers between devices: 534 us -> none  [the longest x99 192 us: matmul(): jnp.dot(a, w, preferred_element_type=jnp.float32).astype(jnp.bfloat16)]
    dot_general x122 -> x17, matrix products: 640 us -> 240 us  [dot(): return lax.dot_general(a, b, (dims, ((), ())), preferred_element_type=F32)]
    all_gather x0 -> x6, waiting for transfers between devices: none -> 269 us  [gather(): return lax.all_gather(w, 'dp', axis=0, tiled=True)]
    dot_general x192 -> x0, other arithmetic: 233 us -> none
    dot_general x231 -> x0, waiting for transfers between devices: 206 us -> none  [the longest x99 196 us: matmul(): jnp.dot(a, w, preferred_element_type=jnp.float32).astype(jnp.bfloat16)]
    dot_general x114 -> x0, local copies, waits for them, and re-layouts: 60.1 us -> none  [the longest x34 43.4 us: matmul(): jnp.dot(a, w, preferred_element_type=jnp.float32).astype(jnp.bfloat16)]
    squeeze x5 -> x0, waiting for transfers between devices: 58.4 us -> none  [stack(): h = layer(h, {name: w[number] for name, w in weights.items()})]
  transfers between devices with their start and end apart: 236 -> 13, of which waited for: 65 -> 11; matrix products, arithmetic and copies ran while one was open for 51% -> 22% of each run, Pallas kernels for 0% -> 0%
where the time goes in v1:
time: 1290 us
  waiting for transfers between devices  916 us (71%)
  matrix products  240 us (19%)
  local copies, waits for them, and re-layouts  85.9 us (7%)
  between operations  14.9 us (1%)
  other arithmetic  14.1 us (1%)
    reduce_scatter x6, waiting for transfers between devices, scatter(): return lax.psum_scatter(g, 'dp', scatter_dimension=0, tiled=True)  646 us
    all_gather x6, waiting for transfers between devices, gather(): return lax.all_gather(w, 'dp', axis=0, tiled=True)  269 us
    dot_general x17, matrix products, dot(): return lax.dot_general(a, b, (dims, ((), ())), preferred_element_type=F32)  240 us
    reshape x8, local copies, waits for them, and re-layouts, apart(): t = g.reshape(-1, 80, GROUP, 640).transpose(0, 2, 1, 3)  37 us
  transfers between devices with their start and end apart: 13, of which 11 were waited for; matrix products, arithmetic and copies ran while one was open for 22% of the time, Pallas kernels for 0%

profile of v1, /device:TPU:0, one launch (start us, length us, event | category | flops | bytes accessed | tf_op | source)
XLA Modules:
  0.0 1287.8 jit_solution(2349022667522828148)
XLA Ops:
  7.2 1.5 pad_maximum_fusion
  9.1 11.7 all_to_all.10
  20.8 1.9 slice_reduce_fusion
  25.7 0.7 fusion.51
  27.6 3.0 copy.53
  31.2 0.9 copy-done.16
  32.1 51.4 %all-gather.9.cloned.1.call-done = bf16[2560,640]{1,0:T(8,128)(2,1)} async-done(((bf16[80,640]{1,0:T(8,128)(2,1)}), bf16[2560,640]{1,0:T(8,128)(2,1)}) %all-gather.9.cloned.1.call-update) | async-done | bytes 3276816 | tf_op jit(solution)/shard_map/all_gather | solution.py:30
  83.5 3.3 copy.55
  86.8 2.2 copy.73
  88.9 56.1 %all-gather.11.cloned.1.call-done = bf16[2560,640]{1,0:T(8,128)(2,1)} async-done(((bf16[80,640]{1,0:T(8,128)(2,1)}), bf16[2560,640]{1,0:T(8,128)(2,1)}) %all-gather.11.cloned.1.call-update) | async-done | bytes 3276816 | tf_op jit(solution)/shard_map/all_gather | solution.py:30
  145.1 3.4 copy.56
  148.5 2.2 copy.74
  150.8 11.9 fusion.46
  162.7 20.4 %multiply_convert_fusion.1 = (bf16[2048,2560]{1,0:T(8,128)(2,1)}, f32[2048,2560]{1,0:T(8,128)}) fusion(f32[2048,2560]{1,0:T(8,128)} %fusion.46, bf16[640,2560]{1,0:T(8,128)(2,1)} %bitcast.122, bf16[1,2048,640]{2,1,0:T(8,128)(2,1)} %param.5, f32[2048]{0:T(1024)S(1)} %add_rsqrt_fusion.1), kind=kOutput, calls=%fused_computation.13 | convolution fusion | flops 6746275840 | bytes 58335232 | tf_op jit(solution)/shard_map/dot_general | solution.py:12
  183.1 23.1 %all-gather.13.cloned.1.call-done = bf16[2560,640]{1,0:T(8,128)(2,1)} async-done(((bf16[80,640]{1,0:T(8,128)(2,1)}), bf16[2560,640]{1,0:T(8,128)(2,1)}) %all-gather.13.cloned.1.call-update) | async-done | bytes 3276816 | tf_op jit(solution)/shard_map/all_gather | solution.py:30
  206.1 3.3 copy.57
  209.4 2.2 copy.75
  211.7 55.4 %all-gather.15.cloned.1.call-done = bf16[2560,640]{1,0:T(8,128)(2,1)} async-done(((bf16[80,640]{1,0:T(8,128)(2,1)}), bf16[2560,640]{1,0:T(8,128)(2,1)}) %all-gather.15.cloned.1.call-update) | async-done | bytes 3276816 | tf_op jit(solution)/shard_map/all_gather | solution.py:30
  267.0 3.3 copy.58
  270.3 2.2 copy.76
  272.5 56.0 %all-gather.19.cloned.1.call-done = bf16[1,2560,640]{2,1,0:T(8,128)(2,1)} async-done(((bf16[1,80,640]{2,1,0:T(8,128)(2,1)}), bf16[1,2560,640]{2,1,0:T(8,128)(2,1)}) %all-gather.19.cloned.1.call-update) | async-done | bytes 3276816 | tf_op jit(solution)/shard_map/all_gather | solution.py:30
  328.5 11.1 fusion.16
  339.7 11.5 fusion.42
  351.2 11.4 fusion.40
  362.7 27.3 %all-gather.17.cloned.1.call-done = bf16[1,2560,640]{2,1,0:T(8,128)(2,1)} async-done(((bf16[1,80,640]{2,1,0:T(8,128)(2,1)}), bf16[1,2560,640]{2,1,0:T(8,128)(2,1)}) %all-gather.17.cloned.1.call-update) | async-done | bytes 3276816 | tf_op jit(solution)/shard_map/all_gather | solution.py:30
  390.0 29.8 %fusion.2 = (bf16[2048,2560]{1,0:T(8,128)(2,1)}, bf16[2048,2560]{1,0:T(8,128)(2,1)}) fusion(f32[2048,2560]{1,0:T(8,128)} %fusion.40, f32[2048,2560]{1,0:T(8,128)} %fusion.42, bf16[1,2560,640]{2,1,0:T(8,128)(2,1)} %all-gather.17.cloned.1.call-done, bf16[1,2048,640]{2,1,0:T(8,128)(2,1)} %param.6), kind=kOutput, calls=%fused_computation.6 | convolution fusion | flops 6789529600 | bytes 68812800 | tf_op jit(solution)/shard_map/dot_general | solution.py:12
  419.7 10.8 convolution_convert_fusion.5
  430.5 5.6 reshape.147
  436.1 2.2 copy.60
  438.4 5.2 copy.52
  443.6 10.9 convolution_convert_fusion.3
  454.5 5.6 reshape.151
  460.1 2.2 copy.62
  462.3 0.9 copy-done.9
  463.2 9.9 fusion.52
  473.2 8.4 fusion.18
  481.7 4.5 fusion.31
  486.2 27.3 %fusion.5 = (bf16[2048,2560]{1,0:T(8,128)(2,1)}, bf16[2048,2560]{1,0:T(8,128)(2,1)}) fusion(f32[2048,2560]{1,0:T(8,128)} %fusion.46, f32[2048,2560]{1,0:T(8,128)} %get-tuple-element.37, bf16[2048,640]{0,1:T(8,128)(2,1)S(1)} %fusion.31, bf16[1,2560,640]{2,1,0:T(8,128)(2,1)S(1)} %copy-done.22), kind=kOutput, calls=%fused_computation.9 | convolution fusion | flops 6789529600 | bytes 68812800 | tf_op jit(solution)/shard_map/dot_general | solution.py:12
  513.6 10.9 convolution_convert_fusion.6
  524.5 6.7 reshape.145
  531.1 4.0 copy.59
  535.2 10.9 convolution_convert_fusion.4
  546.1 6.7 reshape.149
  552.8 4.1 copy.61
  557.0 13.3 %convolution_convert_fusion.2 = bf16[2560,640]{1,0:T(8,128)(2,1)} fusion(bf16[2048,2560]{1,0:T(8,128)(2,1)} %get-tuple-element.36, bf16[2048,640]{0,1:T(8,128)(2,1)} %copy-done.2), kind=kOutput, calls=%fused_computation.43 | convolution fusion | flops 6712524800 | bytes 16384000 | tf_op jit(solution)/shard_map/dot_general | solution.py:12
  570.4 19.8 %fusion.19 = bf16[2560,640]{1,0:T(8,128)(2,1)} fusion(f32[2048,2560]{1,0:T(8,128)} %fusion.42, f32[2048,2560]{1,0:T(8,128)} %fusion.40, bf16[1,2048,640]{2,1,0:T(8,128)(2,1)} %param.6), kind=kOutput, calls=%fused_computation.42 | convolution fusion | flops 6743982080 | bytes 47841280 | tf_op jit(solution)/shard_map/dot_general | solution.py:12
  590.2 10.8 fusion.53
  601.1 10.9 fusion.14
  612.0 0.9 stack.25
  612.9 104.8 %reduce-scatter.13.cloned.1.call-done = bf16[80,640]{1,0:T(8,128)(2,1)} async-done(((bf16[2560,640]{1,0:T(8,128)(2,1)}), bf16[80,640]{1,0:T(8,128)(2,1)}) %reduce-scatter.13.cloned.1.call-update) | async-done | bytes 102416 | tf_op jit(solution)/shard_map/reduce_scatter | solution.py:34
  717.7 0.9 stack.27
  718.7 139.1 %reduce-scatter.7.cloned.1.call-done = bf16[80,640]{1,0:T(8,128)(2,1)} async-done(((bf16[2560,640]{1,0:T(8,128)(2,1)}), bf16[80,640]{1,0:T(8,128)(2,1)}) %reduce-scatter.7.cloned.1.call-update) | async-done | bytes 102416 | tf_op jit(solution)/shard_map/reduce_scatter | solution.py:34
  857.7 0.9 stack.24
  858.6 138.9 %reduce-scatter.11.cloned.1.call-done = bf16[80,640]{1,0:T(8,128)(2,1)} async-done(((bf16[2560,640]{1,0:T(8,128)(2,1)}), bf16[80,640]{1,0:T(8,128)(2,1)}) %reduce-scatter.11.cloned.1.call-update) | async-done | bytes 102416 | tf_op jit(solution)/shard_map/reduce_scatter | solution.py:34
  997.5 0.9 stack.26
  998.6 1.0 copy.63
  999.5 3.7 all-to-all-start.1
  1003.2 5.8 fusion.30
  1009.1 4.4 copy.66
  1013.4 124.5 %reduce-scatter.15.cloned.1.call-done = bf16[80,640]{1,0:T(8,128)(2,1)} async-done(((bf16[2560,640]{1,0:T(8,128)(2,1)}), bf16[80,640]{1,0:T(8,128)(2,1)}) %reduce-scatter.15.cloned.1.call-update) | async-done | bytes 102416 | tf_op jit(solution)/shard_map/reduce_scatter | solution.py:34
  1137.9 139.2 %reduce-scatter.17.cloned.1.call-done = bf16[80,640]{1,0:T(8,128)(2,1)} async-done(((bf16[2560,640]{1,0:T(8,128)(2,1)}), bf16[80,640]{1,0:T(8,128)(2,1)}) %reduce-scatter.17.cloned.1.call-update) | async-done | bytes 102416 | tf_op jit(solution)/shard_map/reduce_scatter | solution.py:34
  1277.1 1.6 pad_maximum_fusion.1
  1279.0 0.8 copy.71
  1279.9 0.8 copy.72
  (90 shorter events, 5.8 us)
Async XLA Ops:
  7.2 18.6 %copy-start.15 = (bf16[2,80,640]{2,1,0:T(8,128)(2,1)S(1)}, bf16[2,80,640]{2,1,0:T(8,128)(2,1)}, u32[]{:S(2)}) copy-start(bf16[2,80,640]{2,1,0:T(8,128)(2,1)} %param.9) | copy-start | bytes 614404
  7.2 76.3 %all-gather.9.cloned.1.call-start = ((), (), s32[]{:S(2)}) async-start(), calls=%async_computation.8 | async-start | bytes 3379200 | tf_op jit(solution)/shard_map/all_gather | solution.py:30
  23.4 121.6 %all-gather.11.cloned.1.call-start = ((), (), s32[]{:S(2)}) async-start(), calls=%async_computation.9 | async-start | bytes 3379200 | tf_op jit(solution)/shard_map/all_gather | solution.py:30
  24.2 181.9 %all-gather.13.cloned.1.call-start = ((), (), s32[]{:S(2)}) async-start(), calls=%async_computation.10 | async-start | bytes 3379200 | tf_op jit(solution)/shard_map/all_gather | solution.py:30
  24.9 242.1 %all-gather.15.cloned.1.call-start = ((), (), s32[]{:S(2)}) async-start(), calls=%async_computation.11 | async-start | bytes 3379200 | tf_op jit(solution)/shard_map/all_gather | solution.py:30
  25.7 302.8 %all-gather.19.cloned.1.call-start = ((), (), s32[]{:S(2)}) async-start(), calls=%async_computation.19 | async-start | bytes 3379200 | tf_op jit(solution)/shard_map/all_gather | solution.py:30
  26.5 363.5 %all-gather.17.cloned.1.call-start = ((), (), s32[]{:S(2)}) async-start(), calls=%async_computation.18 | async-start | bytes 3379200 | tf_op jit(solution)/shard_map/all_gather | solution.py:30
  27.0 585.0 %reduce-scatter.9.cloned.1.call-start = ((), (), s32[]{:S(2)}) async-start(), calls=%async_computation.13 | async-start | bytes 3379200 | tf_op jit(solution)/shard_map/reduce_scatter | solution.py:34
  30.6 297.9 %copy-start = (bf16[1,2048,640]{1,2,0:T(8,128)(2,1)}, bf16[1,2048,640]{1,2,0:T(8,128)(2,1)S(1)}, u32[]{:S(2)}) copy-start(bf16[1,2048,640]{1,2,0:T(8,128)(2,1)S(1)} %copy.53) | copy-start | bytes 7864324
  31.2 0.9 copy-start.16
  32.1 130.6 %copy-start.18 = (f32[2048]{0:T(1024)}, f32[2048]{0:T(1024)S(1)}, u32[]{:S(2)}) copy-start(f32[2048]{0:T(1024)S(1)} %add_rsqrt_fusion.1) | copy-start | bytes 24580
  145.1 5.7 copy-start.4
  145.1 5.7 copy-start.14
  328.5 11.2 copy-start.6
  339.6 11.6 copy-start.20
  339.6 11.6 copy-start.10
  339.7 11.6 copy-start.8
  362.7 57.0 %copy-start.11 = (bf16[2048,640]{0,1:T(8,128)(2,1)S(1)}, bf16[2048,640]{0,1:T(8,128)(2,1)}, u32[]{:S(2)}) copy-start(bf16[2048,640]{0,1:T(8,128)(2,1)} %copy-done.10) | copy-start | bytes 7864324
  438.3 5.3 copy-start.12
  438.4 279.4 %reduce-scatter.13.cloned.1.call-start = ((), (), s32[]{:S(2)}) async-start(), calls=%async_computation.15 | async-start | bytes 3379200 | tf_op jit(solution)/shard_map/reduce_scatter | solution.py:34
  460.1 3.1 copy-start.9
  460.1 13.1 %slice-start = ((s8[10485760]{0:T(1024)(128)(4,1)}), s8[4194304]{0:T(1024)(128)(4,1)S(1)}, s32[]{:S(2)}) async-start(s8[10485760]{0:T(1024)(128)(4,1)} %bitcast.138), calls=%async_computation.20 | async-start | bytes 8388608
  463.2 10.0 copy-start.7
  463.2 10.0 copy-start.13
  463.2 10.0 slice-start.1
  463.2 10.0 slice-start.2
  473.2 8.4 copy-start.21
  473.2 8.5 copy-start.3
  481.7 376.1 %reduce-scatter.7.cloned.1.call-start = ((), (), s32[]{:S(2)}) async-start(), calls=%async_computation.12 | async-start | bytes 3379200 | tf_op jit(solution)/shard_map/reduce_scatter | solution.py:34
  481.7 4.5 copy-start.22
  486.2 27.3 %copy-start.2 = (bf16[2048,640]{0,1:T(8,128)(2,1)}, bf16[2048,640]{0,1:T(8,128)(2,1)S(1)}, u32[]{:S(2)}) copy-start(bf16[2048,640]{0,1:T(8,128)(2,1)S(1)} %fusion.31) | copy-start | bytes 7864324
  486.2 27.3 %copy-start.1 = (bf16[1,2048,640]{1,2,0:T(8,128)(2,1)S(1)}, bf16[1,2048,640]{1,2,0:T(8,128)(2,1)}, u32[]{:S(2)}) copy-start(bf16[1,2048,640]{1,2,0:T(8,128)(2,1)} %copy-done) | copy-start | bytes 7864324
  486.2 27.3 %copy-start.19 = (f32[2048]{0:T(1024)S(1)}, f32[2048]{0:T(1024)}, u32[]{:S(2)}) copy-start(f32[2048]{0:T(1024)} %copy-done.18) | copy-start | bytes 24580
  535.2 462.3 %reduce-scatter.11.cloned.1.call-start = ((), (), s32[]{:S(2)}) async-start(), calls=%async_computation.14 | async-start | bytes 3379200 | tf_op jit(solution)/shard_map/reduce_scatter | solution.py:34
  557.0 580.9 %reduce-scatter.15.cloned.1.call-start = ((), (), s32[]{:S(2)}) async-start(), calls=%async_computation.16 | async-start | bytes 3379200 | tf_op jit(solution)/shard_map/reduce_scatter | solution.py:34
  570.4 706.7 %reduce-scatter.17.cloned.1.call-start = ((), (), s32[]{:S(2)}) async-start(), calls=%async_computation.17 | async-start | bytes 3379200 | tf_op jit(solution)/shard_map/reduce_scatter | solution.py:34
  590.2 10.8 copy-start.5
  601.1 10.9 copy-start.17
  999.5 279.2 %all-to-all-start.1 = ((bf16[4,4,20,640]{3,1,2,0:T(4,128)(2,1)}), bf16[4,4,20,640]{3,1,2,0:T(4,128)(2,1)S(1)}, u32[]{:S(2)}, u32[]{:S(2)}) async-start(bf16[4,4,20,640]{3,1,2,0:T(4,128)(2,1)} %copy.63), calls=%async_computation.5 | async-start | bytes 819200 | tf_op jit(solution)/shard_map/all_to_all | solution.py:26
Sparse Core Ops, SparseCore 0:
  23.6 59.8 all-gather.8
  86.9 58.1 all-gather.10
  147.9 58.1 all-gather.12
  208.8 58.1 all-gather.14
  270.3 58.1 all-gather.18
  331.8 58.1 all-gather.16
  438.5 139.4 reduce-scatter.8
  580.3 137.3 reduce-scatter.12
  720.0 137.6 reduce-scatter.6
  859.8 137.6 reduce-scatter.10
  999.8 138.0 reduce-scatter.14
  1140.1 136.9 reduce-scatter.16

commit v2 on v1

v2 whole, which is shorter than its diff:
```python
import functools

import jax
import jax.numpy as jnp
from jax import lax
from jax.experimental import pallas as pl
from jax.experimental.pallas import tpu as pltpu
from jax.sharding import PartitionSpec as P

LAYERS = 2
BF = jnp.bfloat16
F32 = jnp.float32
D = 640
FF = 2560
ROWS = 80
CH = 5
LN = 128
FC = 512
GROUP = 4
SLOTS = 4
NN = ((1,), (0,))
NT = ((1,), (1,))


def aligned(i, n):
    return i if isinstance(i, int) else pl.multiple_of(i, n)


def dot(a, b, dims):
    return lax.dot_general(a, b, (dims, ((), ())), preferred_element_type=F32)


def exchange(t):
    n = lax.axis_size("dp")
    groups = [[g + i for i in range(GROUP)] for g in range(0, n, GROUP)]
    return lax.all_to_all(t, "dp", 0, 0, axis_index_groups=groups, tiled=True)


def rows_to_blocks(w):
    m, r, f = w.shape
    t = w.reshape(m, r, GROUP, f // GROUP).transpose(2, 0, 1, 3)
    t = exchange(t)
    return t.transpose(1, 0, 2, 3).reshape(m, GROUP * r, f // GROUP)


def blocks_to_rows(b):
    m, r, f = b.shape
    t = b.reshape(m, GROUP, r // GROUP, f).transpose(1, 0, 2, 3)
    t = exchange(t)
    return t.transpose(1, 2, 0, 3).reshape(m, r // GROUP, GROUP * f)


def kernel(mt, wblk, x_hbm, dy_hbm, out_x, out_gu, out_d,
           W, h, ct, a, aT, ctT, acc, E, R1, R2, R3, R4, S2, S3, S4,
           R1d, R2d, R3d, R4d, S2d, S3d, S4d, lsem, ag_s, ag_r, rs_s, rs_r, rd_s, rd_r):
    T = x_hbm.shape[0]
    tiles = T // mt
    me = lax.axis_index("dp")
    c = me % 2
    z = (me // 2) % 4
    zl = z % 2
    zh = z // 2
    y = (me // 8) % 2
    x = me // 16
    b = me // 2
    nc = 1 - c
    nx = 1 - x
    ny = 1 - y

    def dev(x_, y_, z_, c_):
        return {"dp": ((x_ * 2 + y_) * 4 + z_) * 2 + c_}

    d_core = dev(x, y, z, nc)
    d_x = dev(nx, y, z, c)
    d_y = dev(x, ny, z, c)
    zs = [(z + k) % 4 for k in (1, 2, 3)]
    d_z = [dev(x, y, zz, c) for zz in zs]
    everyone = [d_core, d_x, d_y, *d_z]

    loads = [pltpu.make_async_copy(wblk.at[i], W.at[i, b, c], lsem.at[i]) for i in range(6)]
    loads.append(pltpu.make_async_copy(x_hbm, h, lsem.at[6]))
    loads.append(pltpu.make_async_copy(dy_hbm, ct, lsem.at[7]))
    for i in (2, 0, 1, 5, 3, 4, 6, 7):
        loads[i].start()

    barrier = pltpu.get_barrier_semaphore()
    for d in everyone:
        pl.semaphore_signal(barrier, inc=1, device_id=d, device_id_type=pl.DeviceIdType.MESH)
    pl.semaphore_wait(barrier, len(everyone))

    msgs = [(2, 1, 0, D), (0, 2, 0, 256), (0, 2, 256, 256), (0, 2, 512, 128), (5, 1, 0, D), (3, 2, 0, 256), (3, 2, 256, 384)]
    used = [0]

    def part(msg, first, n):
        m, k, lo, w = msg
        return W.at[pl.ds(m, k), pl.ds(first, n), c, :, pl.ds(lo, w)]

    def push(msg, first, n, d):
        i = used[0]
        used[0] += 1
        ref = part(msg, first, n)
        cp = pltpu.make_async_remote_copy(src_ref=ref, dst_ref=ref, send_sem=ag_s.at[i], recv_sem=ag_r.at[i],
                                          device_id=d, device_id_type=pl.DeviceIdType.MESH)
        return cp

    def start(copies):
        for cp in copies:
            cp.start()

    zc, xy, yx, cc = [], [], [], []
    base = 8 * x + 4 * y
    for g in msgs:
        zc.append([push(g, b, 1, d) for d in d_z])
        xy.append([push(g, base, 2, d_x), push(g, base + 2, 2, d_y)])
        yx.append([push(g, 4 * y, 2, d_y), push(g, 8 + 4 * y, 2, d_y), push(g, 8 * x + 2, 2, d_x), push(g, 8 * x + 6, 2, d_x)])
        cc.append([push(g, base, 4, d_core), push(g, 8 * nx + 4 * y, 2, d_core), push(g, 8 * x + 4 * ny + 2, 2, d_core),
                   push(g, 4 * ny, 2, d_core), push(g, 8 + 4 * ny, 2, d_core), push(g, 8 * nx + 2, 2, d_core), push(g, 8 * nx + 6, 2, d_core)])

    def st_z(i):
        start(zc[i])

    def st_xy(i):
        for cp in zc[i]:
            cp.wait_recv()
        start(xy[i])
        start(cc[i][:1])

    def st_yx(i):
        for cp in xy[i]:
            cp.wait_recv()
        start(yx[i])
        start(cc[i][1:3])

    def st_c(i):
        for cp in yx[i]:
            cp.wait_recv()
        start(cc[i][3:])

    def st_done(i):
        for cp in cc[i]:
            cp.wait_recv()
        for cp in (*zc[i], *xy[i], *yx[i], *cc[i]):
            cp.wait_send()

    def tick(k):
        if 0 <= k < len(msgs):
            st_xy(k)
        if 0 <= k - 1 < len(msgs):
            st_yx(k - 1)
        if 0 <= k - 2 < len(msgs):
            st_c(k - 2)
        if 0 <= k - 3 < len(msgs):
            st_done(k - 3)

    for i in range(6):
        loads[i].wait()
    for i in range(len(msgs)):
        st_z(i)

    def row_tile(i):
        return pl.ds(aligned(i * mt, mt), mt)

    def norm_tile(i, with_ct):
        rows = row_tile(i)
        wide = h[rows, :].astype(F32)
        scale = lax.rsqrt(jnp.mean(wide * wide, -1, keepdims=True) + 1e-6)
        v = (wide * scale).astype(BF)
        a[rows, :] = v
        aT[:, rows] = v.T
        if with_ct:
            ctT[:, rows] = ct[rows, :].T
        acc[rows, :] = jnp.zeros((mt, D), F32)

    def norm_all(with_ct):
        @pl.loop(0, tiles)
        def _(i):
            norm_tile(i, with_ct)

    def lanes(s):
        return pl.ds(aligned(s * LN, LN), LN)

    def columns(m, s):
        cols = []
        for q in range(4):
            cols.append(jnp.concatenate([W[m, 2 * g + q // 2, q % 2, :, lanes(s)] for g in range(8)], axis=0))
        return jnp.concatenate(cols, axis=1)

    def down_place(q, t, s):
        j = 8 * s + t
        k = 8 * q + j // 5
        return k // 2, k % 2, pl.ds(aligned((j % 5) * 16, 16), 16)

    def down_rows(m, s):
        rows = []
        for q in range(4):
            for t in range(8):
                b_, c_, r_ = down_place(q, t, s)
                rows.append(W[m, b_, c_, r_, :])
        return jnp.concatenate(rows, axis=0)

    def forward_chunk(s):
        @pl.loop(0, tiles)
        def _(i):
            rows = row_tile(i)
            v = a[rows, :]
            g = dot(v, columns(0, s), NN)
            u = dot(v, columns(1, s), NN)
            act = (jax.nn.silu(g) * u).astype(BF)
            acc[rows, :] += dot(act, down_rows(2, s), NN)

    def back_tokens(m, s):
        @pl.loop(0, tiles)
        def _(i):
            rows = row_tile(i)
            v = a[rows, :]
            wg = columns(m, s)
            wu = columns(m + 1, s)
            g = dot(v, wg, NN)
            u = dot(v, wu, NN)
            dact = dot(ct[rows, :], down_rows(m + 2, s), NT).astype(BF).astype(F32)
            sg = jax.nn.sigmoid(g)
            si = g * sg
            E[2, rows, :] = (si * u).astype(BF)
            du = (dact * si).astype(BF)
            dg = (dact * u * (sg * (1 + g * (1 - sg)))).astype(BF)
            E[0, rows, :] = dg
            E[1, rows, :] = du
            acc[rows, :] += dot(dg, wg, NT) + dot(du, wu, NT)

    def back_weights(m, s):
        for j in range(2):
            r = dot(aT[...], E[j], NN).astype(BF)
            for q in range(4):
                for g in range(8):
                    W[m + j, 2 * g + q // 2, q % 2, :, lanes(s)] = r[ROWS * g:ROWS * (g + 1), LN * q:LN * (q + 1)]
        r = dot(ctT[...], E[2], NN).astype(BF).T
        for q in range(4):
            for t in range(8):
                b_, c_, r_ = down_place(q, t, s)
                W[m + 2, b_, c_, r_, :] = r[LN * q + 16 * t:LN * q + 16 * (t + 1), :]

    def back_norm(out):
        @pl.loop(0, tiles)
        def _(i):
            rows = row_tile(i)
            wide = h[rows, :].astype(F32)
            scale = lax.rsqrt(jnp.mean(wide * wide, -1, keepdims=True) + 1e-6)
            da = acc[rows, :].astype(BF).astype(F32)
            inner = jnp.mean(da * wide, -1, keepdims=True)
            dh = (da * scale - wide * (scale * scale * scale * inner)).astype(BF)
            out[rows, :] = (ct[rows, :].astype(F32) + dh.astype(F32)).astype(BF)

    def rcopy(src, dst, d, ss, rr):
        return pltpu.make_async_remote_copy(src_ref=src, dst_ref=dst, send_sem=ss, recv_sem=rr,
                                            device_id=d, device_id_type=pl.DeviceIdType.MESH)

    class Reduce:
        def __init__(self, m, n, ln, slot, bufs, ss, rr):
            self.m, self.n, self.ln = m, n, ln
            self.r1, self.r2, self.r3, self.r4, self.s2, self.s3, self.s4 = bufs
            self.slot = slot
            self.c1 = rcopy(W.at[pl.ds(m, n), :, nc, :, ln], self.r1.at[slot], d_core, ss.at[slot, 0], rr.at[slot, 0])
            self.c2 = [rcopy(self.s2.at[k], self.r2.at[slot, k], (d_y, d_x)[k], ss.at[slot, 1 + k], rr.at[slot, 1 + k]) for k in (0, 1)]
            self.c3 = [rcopy(self.s3.at[k], self.r3.at[slot, k], (d_x, d_y)[k], ss.at[slot, 3 + k], rr.at[slot, 3 + k]) for k in (0, 1)]
            self.c4 = [rcopy(self.s4.at[k], self.r4.at[slot, k], d_z[k], ss.at[slot, 5 + k], rr.at[slot, 5 + k]) for k in range(3)]

        def two(self, j, b_):
            return W[self.m + j, b_, c, :, self.ln].astype(F32) + self.r1[self.slot, j, b_].astype(F32)

        def send1(self):
            self.c1.start()

        def send2(self):
            self.c1.wait()
            for j in range(self.n):
                for k in range(2):
                    for l in range(2):
                        self.s2[0, j, 2 * k + l] = self.two(j, 8 * k + 4 * ny + l).astype(BF)
                        self.s2[1, j, 2 * k + l] = self.two(j, 8 * nx + 4 * k + 2 + l).astype(BF)
            for cp in self.c2:
                cp.start()

        def send3(self):
            for cp in self.c2:
                cp.wait()
            for j in range(self.n):
                for l in range(2):
                    v = self.two(j, 8 * nx + 4 * y + l) + self.r2[self.slot, 0, j, 2 * nx + l].astype(F32)
                    self.s3[0, j, l] = v.astype(BF)
                    v = self.two(j, 8 * x + 4 * ny + 2 + l) + self.r2[self.slot, 1, j, 2 * ny + l].astype(F32)
                    self.s3[1, j, l] = v.astype(BF)
            for cp in self.c3:
                cp.start()

        def four(self, j, z_):
            h_ = z_ // 2
            l_ = z_ % 2
            v = self.two(j, 8 * x + 4 * y + z_)
            v += self.r2[self.slot, h_, j, 2 * (x * (1 - h_) + y * h_) + l_].astype(F32)
            return v + self.r3[self.slot, h_, j, l_].astype(F32)

        def send4(self):
            for cp in self.c3:
                cp.wait()
            for j in range(self.n):
                for k in range(3):
                    self.s4[k, j] = self.four(j, zs[k]).astype(BF)
            for cp in self.c4:
                cp.start()

        def finish(self, store):
            for cp in self.c4:
                cp.wait()
            for j in range(self.n):
                v = self.four(j, z)
                for k in range(3):
                    v += self.r4[self.slot, k, j].astype(F32)
                store(j, v.astype(BF))

    gu_bufs = (R1, R2, R3, R4, S2, S3, S4)
    d_bufs = (R1d, R2d, R3d, R4d, S2d, S3d, S4d)

    def layer_of(t):
        return 1 - t // CH

    def gu(t):
        return Reduce(3 * layer_of(t), 2, lanes(t % CH), t % SLOTS, gu_bufs, rs_s, rs_r)

    def dn(t):
        return Reduce(3 * layer_of(t) + 2, 1, pl.ds(0, D), 0, d_bufs, rd_s, rd_r)

    def store_gu(t):
        l = layer_of(t)

        def f(j, v):
            out_gu[l, j, :, lanes(t % CH)] = v
        return f

    def store_d(t):
        l = layer_of(t)

        def f(j, v):
            out_d[l] = v
        return f

    def both(t, lo, f):
        @pl.when((t >= 0) & (t < 2 * CH))
        def _():
            f(gu(t), store_gu(t))

            @pl.when(t % CH == CH - 1)
            def _():
                f(dn(t), store_d(t))

    tick(0)
    tick(1)
    loads[6].wait()
    loads[7].wait()
    norm_all(True)
    tick(2)
    tick(3)
    tick(4)

    @pl.loop(0, 2)
    def _(s):
        forward_chunk(s)

    tick(5)

    @pl.loop(2, 4)
    def _(s):
        forward_chunk(s)

    tick(6)
    forward_chunk(4)

    @pl.loop(0, tiles)
    def _(i):
        rows = row_tile(i)
        h[rows, :] = (h[rows, :].astype(F32) + acc[rows, :].astype(BF).astype(F32)).astype(BF)

    norm_all(False)
    st_yx(6)
    st_c(5)
    st_done(4)
    st_done(5)

    @pl.loop(0, 2 * CH + 2)
    def _(t):
        m = 3 * (1 - t // CH)
        s = t % CH

        @pl.when(t == 1)
        def _():
            st_c(6)

        @pl.when(t == 2)
        def _():
            st_done(6)

        @pl.when(t < 2 * CH)
        def _():
            back_tokens(m, s)

        both(t - 1, 0, lambda r, st: r.send2())
        both(t - 2, 0, lambda r, st: r.send4())

        @pl.when(t < 2 * CH)
        def _():
            back_weights(m, s)

        both(t, 0, lambda r, st: r.send1())
        both(t - 1, 0, lambda r, st: r.send3())
        both(t - 2, 0, lambda r, st: r.finish(st))

        @pl.when(t == CH - 1)
        def _():
            back_norm(ct)
            again = pltpu.make_async_copy(x_hbm, h, lsem.at[6])
            again.start()
            again.wait()
            norm_all(True)

        @pl.when(t == 2 * CH - 1)
        def _():
            back_norm(out_x)


def step(x, dy, wg, wu, wd):
    t = x.shape[1]
    mt = min(512, t)
    mine = rows_to_blocks(jnp.concatenate([wg, wu]))
    wblk = jnp.stack([mine[0], mine[2], wd[0], mine[1], mine[3], wd[1]])
    ag = 16 * 7
    dma = pltpu.SemaphoreType.DMA

    def v(*shape, dtype=BF):
        return pltpu.VMEM(shape, dtype)

    def rs_bufs(slots, n, w):
        r = [v(slots, n, 16, ROWS, w), v(slots, 2, n, 4, ROWS, w), v(slots, 2, n, 2, ROWS, w), v(slots, 3, n, ROWS, w)]
        return r, [v(2, n, 4, ROWS, w), v(2, n, 2, ROWS, w), v(3, n, ROWS, w)]

    gr, gs = rs_bufs(SLOTS, 2, LN)
    dr, ds_ = rs_bufs(1, 1, D)
    vm = pl.BlockSpec(memory_space=pltpu.VMEM)
    hbm = pl.BlockSpec(memory_space=pl.ANY)
    flops = 22 * 2 * t * D * FF
    out_x, out_gu, out_d = pl.pallas_call(
        functools.partial(kernel, mt),
        out_shape=(jax.ShapeDtypeStruct((t, D), BF), jax.ShapeDtypeStruct((LAYERS, 2, ROWS, D), BF), jax.ShapeDtypeStruct((LAYERS, ROWS, D), BF)),
        in_specs=[hbm, hbm, hbm],
        out_specs=(vm, vm, vm),
        scratch_shapes=[
            v(6, 16, 2, ROWS, D), v(t, D), v(t, D), v(t, D), v(D, t), v(D, t), v(t, D, dtype=F32), v(3, t, FC),
            *gr, *gs, *dr, *ds_,
            dma((8,)), dma((ag,)), dma((ag,)), dma((SLOTS, 8)), dma((SLOTS, 8)), dma((1, 8)), dma((1, 8)),
        ],
        compiler_params=pltpu.CompilerParams(collective_id=0, has_side_effects=True, vmem_limit_bytes=67043328),
        cost_estimate=pl.CostEstimate(flops=flops, bytes_accessed=40_000_000, transcendentals=0),
        name="stack",
    )(wblk, x[0], dy[0])
    back = blocks_to_rows(out_gu.transpose(1, 0, 2, 3).reshape(2 * LAYERS, ROWS, D))
    return out_x[None], back[:LAYERS], back[LAYERS:], out_d


def solution(mesh):
    w = P(None, "dp", None)
    t = P(("rep", "dp"), None, None)
    o = P("rep", "dp", None)
    return jax.shard_map(step, mesh=mesh, in_specs=(t, t, w, w, w), out_specs=(t, o, o, o), check_vma=False)
```

time: 1290 us -> 350 us (0.27)
  waiting for transfers between devices: 916 us -> 7.37 us
  Pallas kernels: 0 us -> 315 us
  matrix products: 240 us -> 0 us
  local copies, waits for them, and re-layouts: 85.9 us -> 9.77 us
  between operations: 14.9 us -> 0.77 us
    reduce_scatter x6 -> x0, waiting for transfers between devices: 646 us -> none  [scatter(): return lax.psum_scatter(g, 'dp', scatter_dimension=0, tiled=True)]
    pallas_call x0 -> x1, Pallas kernels: none -> 315 us  [step(): pl.pallas_call(functools.partial(kernel, mt), out_shape=(jax.ShapeDtypeSt...]
    all_gather x6 -> x0, waiting for transfers between devices: 269 us -> none  [gather(): return lax.all_gather(w, 'dp', axis=0, tiled=True)]
    dot_general x17 -> x0, matrix products: 240 us -> none  [dot(): return lax.dot_general(a, b, (dims, ((), ())), preferred_element_type=F32)]
    reshape x12 -> x0, local copies, waits for them, and re-layouts: 50.3 us -> none  [the longest x8 37 us: apart(): t = g.reshape(-1, 80, GROUP, 640).transpose(0, 2, 1, 3)]
    unnamed x60 -> x16, local copies, waits for them, and re-layouts: 23.7 us -> 3.37 us
  transfers between devices with their start and end apart: 13 -> 1, of which waited for: 11 -> 1; matrix products, arithmetic and copies ran while one was open for 22% -> 0% of each run, Pallas kernels for 0% -> 0%
where the time goes in v2:
time: 350 us; the launch traced here: 349 us
  Pallas kernels  315 us (90%)
  blocking collectives  11.7 us (3%)
  local copies, waits for them, and re-layouts  9.77 us (3%)
  waiting for transfers between devices  7.37 us (2%)
  starting transfers between devices  3.5 us (1%)
    pallas_call x1, Pallas kernels, step(): pl.pallas_call(functools.partial(kernel, mt), out_shape=(jax.ShapeDtypeSt...  315 us
    all_to_all x1, blocking collectives, exchange(): return lax.all_to_all(t, 'dp', 0, 0, axis_index_groups=groups, tiled=True)  11.7 us
    all_to_all x1, waiting for transfers between devices, exchange(): return lax.all_to_all(t, 'dp', 0, 0, axis_index_groups=groups, tiled=True)  7.37 us
  transfers between devices with their start and end apart: 1, of which 1 were waited for; matrix products, arithmetic and copies ran while one was open for 0% of the time, Pallas kernels for 0%

profile of v2, /device:TPU:0, one launch (start us, length us, event | category | flops | bytes accessed | tf_op | source)
XLA Modules:
  0.0 349.3 jit_solution(8115386518452719094)
XLA Ops:
  0.6 1.5 pad_maximum_fusion
  2.1 0.0 copy-start.1
  2.1 0.2 reshape.19
  2.3 0.2 copy.19
  2.4 11.7 %all_to_all.10 = bf16[4,4,20,640]{3,1,2,0:T(4,128)(2,1)S(1)} all-to-all(bf16[4,4,20,640]{3,1,2,0:T(4,128)(2,1)S(1)} %copy.19), channel_id=1, replica_groups={{0,1,2,3},{4,5,6,7},{8,9,10,11},{12,13,14,15},{16,17,18,19},{20,21,22,2..., dimensions={0} | all-to-all | bytes 819200 | tf_op jit(solution)/shard_map/all_to_all | solution.py:36
  14.2 1.9 slice_reduce_fusion
  16.3 0.0 copy-done.1
  16.4 0.0 copy-start.3
  16.4 0.8 copy-done.3
  17.2 314.7 %stack.5 = (bf16[2048,640]{1,0:T(8,128)(2,1)}, bf16[2,2,80,640]{3,2,1,0:T(8,128)(2,1)}, bf16[2,80,640]{2,1,0:T(8,128)(2,1)}) custom-call(bf16[6,80,640]{2,1,0:T(8,128)(2,1)} %copy-done.3, bf16[2048,640]{1,0:T(8,128)(2,1)} %bitcast.25, bf16[2048,640]{1,0:T(8,128)(2,1)} %bitcast.26), custom_call_target="tpu_custom_call" | custom-call | flops 147639500800 | bytes 40000000 | tf_op jit(solution)/shard_map/stack/pallas_call | solution.py:449
  331.9 0.0 copy-start
  331.9 1.5 copy.20
  333.4 0.9 reshape_reshape.3
  334.3 3.5 %all-to-all-start.1 = ((bf16[4,4,20,640]{3,1,2,0:T(4,128)(2,1)}), bf16[4,4,20,640]{3,1,2,0:T(4,128)(2,1)S(1)}, u32[]{:S(2)}, u32[]{:S(2)}) async-start(bf16[4,4,20,640]{3,1,2,0:T(4,128)(2,1)} %bitcast.6), calls=%async_computation.1 | async-start | bytes 819200 | tf_op jit(solution)/shard_map/all_to_all | solution.py:36
  337.8 7.4 %all-to-all-done.1 = bf16[4,4,20,640]{3,1,2,0:T(4,128)(2,1)S(1)} async-done(((bf16[4,4,20,640]{3,1,2,0:T(4,128)(2,1)}), bf16[4,4,20,640]{3,1,2,0:T(4,128)(2,1)S(1)}, u32[]{:S(2)}, u32[]{:S(2)}) %all-to-all-start.1) | async-done | bytes 409632 | tf_op jit(solution)/shard_map/all_to_all | solution.py:36
  345.2 0.3 slice_bitcast_fusion
  345.4 0.8 copy.28
  346.3 0.8 copy.27
  347.1 0.0 copy-done
  347.1 0.0 copy-start.2
  347.1 1.5 copy.36
  348.6 0.0 copy-done.2
  348.6 0.7 copy.37
  (10 shorter events, 0.2 us)
Async XLA Ops:
  2.1 14.2 %copy-start.1 = (bf16[2,80,640]{2,1,0:T(8,128)(2,1)S(1)}, bf16[2,80,640]{2,1,0:T(8,128)(2,1)}, u32[]{:S(2)}) copy-start(bf16[2,80,640]{2,1,0:T(8,128)(2,1)} %param.9) | copy-start | bytes 614404
  16.4 0.8 copy-start.3
  331.9 15.2 %copy-start = (bf16[2048,640]{1,0:T(8,128)(2,1)S(1)}, bf16[2048,640]{1,0:T(8,128)(2,1)}, u32[]{:S(2)}) copy-start(bf16[2048,640]{1,0:T(8,128)(2,1)} %get-tuple-element.7) | copy-start | bytes 7864324
  334.3 10.9 %all-to-all-start.1 = ((bf16[4,4,20,640]{3,1,2,0:T(4,128)(2,1)}), bf16[4,4,20,640]{3,1,2,0:T(4,128)(2,1)S(1)}, u32[]{:S(2)}, u32[]{:S(2)}) async-start(bf16[4,4,20,640]{3,1,2,0:T(4,128)(2,1)} %bitcast.6), calls=%async_computation.1 | async-start | bytes 819200 | tf_op jit(solution)/shard_map/all_to_all | solution.py:36
  347.1 1.5 copy-start.2

commit v3 on v2

v3 whole, which is shorter than its diff:
```python
import jax
import jax.numpy as jnp
from jax import lax
from jax.experimental import pallas as pl
from jax.experimental.pallas import tpu as pltpu
from jax.sharding import PartitionSpec as P

LAYERS = 2
BF = jnp.bfloat16
F32 = jnp.float32
D = 640
FF = 2560
ROWS = 80
CH = 5
LN = 128
FC = 512
GROUP = 4
PIECE = 20
PAD = 32
TILES = 4
SLOTS = 4
NN = ((1,), (0,))
NT = ((1,), (1,))


def aligned(i, n):
    return i if isinstance(i, int) else pl.multiple_of(i, n)


def dot(a, b, dims):
    return lax.dot_general(a, b, (dims, ((), ())), preferred_element_type=F32)


def kernel(wg, wu, wd_hbm, x_hbm, dy_hbm, out_x, out_g, out_u, out_d, gu_hbm, act_hbm,
           W, h, ct, a, aT, ctT, acc, E, G, TD, R1, R2, R3, R4, S2, S3, S4,
           R1d, R2d, R3d, R4d, XS, XR, OB,
           lsem, gsem, esem, ag_s, ag_r, rs_s, rs_r, rd_s, rd_r, xs_s, xs_r, ys_s, ys_r):
    T = x_hbm.shape[0]
    tiles = TILES
    mt = T // tiles
    me = lax.axis_index("dp")
    c = me % 2
    z = (me // 2) % 4
    zl = z % 2
    y = (me // 8) % 2
    x = me // 16
    b = me // 2
    q = me % GROUP
    nc = 1 - c
    nx = 1 - x
    ny = 1 - y

    def dev(x_, y_, z_, c_):
        return {"dp": ((x_ * 2 + y_) * 4 + z_) * 2 + c_}

    d_core = dev(x, y, z, nc)
    d_x = dev(nx, y, z, c)
    d_y = dev(x, ny, z, c)
    zs = [(z + k) % 4 for k in (1, 2, 3)]
    d_z = [dev(x, y, zz, c) for zz in zs]
    qs = [(q + k) % GROUP for k in (1, 2, 3)]
    d_q = [{"dp": me - q + qq} for qq in qs]
    everyone = [d_core, d_x, d_y, *d_z, dev(x, y, z + 1 - 2 * zl, nc)]

    def rcopy(src, dst, d, ss, rr):
        return pltpu.make_async_remote_copy(src_ref=src, dst_ref=dst, send_sem=ss, recv_sem=rr,
                                            device_id=d, device_id_type=pl.DeviceIdType.MESH)

    loads = [pltpu.make_async_copy(wd_hbm.at[l], W.at[3 * l + 2, b, c], lsem.at[l]) for l in range(LAYERS)]
    loads.append(pltpu.make_async_copy(x_hbm, h, lsem.at[2]))
    loads.append(pltpu.make_async_copy(dy_hbm, ct, lsem.at[3]))
    for cp in loads:
        cp.start()
    for qq in range(GROUP):
        for l in range(LAYERS):
            for j, w in enumerate((wg, wu)):
                XS[qq, 2 * l + j] = jnp.zeros((PAD, D), BF)
                XS[qq, 2 * l + j, 0:PIECE, :] = w[l, :, D * qq:D * (qq + 1)]

    barrier = pltpu.get_barrier_semaphore()
    for d in everyone:
        pl.semaphore_signal(barrier, inc=1, device_id=d, device_id_type=pl.DeviceIdType.MESH)
    pl.semaphore_wait(barrier, len(everyone))

    xc = [rcopy(XS.at[qs[k]], XR.at[q], d_q[k], xs_s.at[k], xs_r.at[k]) for k in range(3)]
    for cp in xc:
        cp.start()
    row = lax.broadcasted_iota(jnp.int32, (ROWS, GROUP * PAD), 0)
    col = lax.broadcasted_iota(jnp.int32, (ROWS, GROUP * PAD), 1)
    inside = col % PAD
    pick = jnp.where((inside < PIECE) & (inside + PIECE * (col // PAD) == row), 1.0, 0.0).astype(BF)
    row = lax.broadcasted_iota(jnp.int32, (GROUP * PAD, ROWS), 1)
    col = lax.broadcasted_iota(jnp.int32, (GROUP * PAD, ROWS), 0)
    inside = col % PAD
    place = jnp.where((inside < PIECE) & (inside + PIECE * (col // PAD) == row), 1.0, 0.0).astype(BF)

    msgs = [(2, 1, 0, 128), (2, 1, 128, 512), (0, 2, 0, 256), (0, 2, 256, 256), (0, 2, 512, 128),
            (3, 2, 0, 256), (3, 2, 256, 256), (3, 2, 512, 128), (5, 1, 0, 384), (5, 1, 384, 256)]
    used = [0]

    def part(msg, first, n):
        m, k, lo, w = msg
        return W.at[pl.ds(m, k), pl.ds(first, n), c, :, pl.ds(lo, w)]

    def push(msg, first, n, d):
        i = used[0]
        used[0] += 1
        ref = part(msg, first, n)
        return rcopy(ref, ref, d, ag_s.at[i], ag_r.at[i])

    def start(copies):
        for cp in copies:
            cp.start()

    zc, xy, yx, cc = [], [], [], []
    base = 8 * x + 4 * y
    for g in msgs:
        zc.append([push(g, b, 1, d) for d in d_z])
        xy.append([push(g, base, 2, d_x), push(g, base + 2, 2, d_y)])
        yx.append([push(g, 4 * y, 2, d_y), push(g, 8 + 4 * y, 2, d_y), push(g, 8 * x + 2, 2, d_x), push(g, 8 * x + 6, 2, d_x)])
        cc.append([push(g, base, 4, d_core), push(g, 8 * nx + 4 * y, 2, d_core), push(g, 8 * x + 4 * ny + 2, 2, d_core),
                   push(g, 4 * ny, 2, d_core), push(g, 8 + 4 * ny, 2, d_core), push(g, 8 * nx + 2, 2, d_core), push(g, 8 * nx + 6, 2, d_core)])

    def st_z(i):
        start(zc[i])

    def st_xy(i):
        for cp in zc[i]:
            cp.wait_recv()
        start(xy[i])
        start(cc[i][:1])

    def st_yx(i):
        for cp in xy[i]:
            cp.wait_recv()
        start(yx[i])
        start(cc[i][1:3])

    def st_c(i):
        for cp in yx[i]:
            cp.wait_recv()
        start(cc[i][3:])

    def st_done(i):
        for cp in cc[i]:
            cp.wait_recv()
        for cp in (*zc[i], *xy[i], *yx[i], *cc[i]):
            cp.wait_send()

    def tick(k):
        if 0 <= k < len(msgs):
            st_xy(k)
        if 0 <= k - 1 < len(msgs):
            st_yx(k - 1)
        if 0 <= k - 2 < len(msgs):
            st_c(k - 2)
        if 0 <= k - 3 < len(msgs):
            st_done(k - 3)

    loads[0].wait()
    loads[1].wait()
    st_z(0)
    st_z(1)
    XR[q] = XS[q]
    for cp in xc:
        cp.wait()
    for l in range(LAYERS):
        for j in range(2):
            pieces = XR[:, 2 * l + j].reshape(GROUP * PAD, D)
            W[3 * l + j, b, c] = dot(pick, pieces, NN).astype(BF)
    for i in range(2, len(msgs)):
        st_z(i)

    def row_tile(i):
        return pl.ds(aligned(i * mt, mt), mt)

    def norm_all(with_a, with_t):
        @pl.loop(0, tiles)
        def _(i):
            rows = row_tile(i)
            wide = h[rows, :].astype(F32)
            scale = lax.rsqrt(jnp.mean(wide * wide, -1, keepdims=True) + 1e-6)
            v = (wide * scale).astype(BF)
            if with_a:
                a[rows, :] = v
            if with_t:
                aT[:, rows] = v.T
                ctT[:, rows] = ct[rows, :].T
            acc[rows, :] = jnp.zeros((mt, D), F32)

    def lanes(s):
        return pl.ds(aligned(s * LN, LN), LN)

    def columns(m, s):
        cols = []
        for q in range(4):
            cols.append(jnp.concatenate([W[m, 2 * g + q // 2, q % 2, :, lanes(s)] for g in range(8)], axis=0))
        return jnp.concatenate(cols, axis=1)

    def down_place(q, t, s):
        j = 8 * s + t
        k = 8 * q + j // 5
        return k // 2, k % 2, pl.ds(aligned((j % 5) * 16, 16), 16)

    def down_rows(m, s):
        rows = []
        for q in range(4):
            for t in range(8):
                b_, c_, r_ = down_place(q, t, s)
                rows.append(W[m, b_, c_, r_, :])
        return jnp.concatenate(rows, axis=0)

    def keep(l, n):
        return pltpu.make_async_copy(G.at[n % 2], gu_hbm.at[l, n], gsem.at[n % 2])

    def fetch(n):
        return pltpu.make_async_copy(gu_hbm.at[1 - n // (CH * tiles), n % (CH * tiles)], G.at[n % 2], gsem.at[n % 2])

    def keep_act(s):
        return pltpu.make_async_copy(E.at[s % 2], act_hbm.at[s], esem.at[s % 2])

    def fetch_act(s):
        return pltpu.make_async_copy(act_hbm.at[s], E.at[s % 2], esem.at[s % 2])

    def forward_tile(l, s, i, n):
        rows = row_tile(i)

        @pl.when(n >= 2)
        def _():
            keep(l, n - 2).wait()

        v = a[rows, :]
        g = dot(v, columns(3 * l, s), NN)
        u = dot(v, columns(3 * l + 1, s), NN)
        G[n % 2, 0] = g
        G[n % 2, 1] = u
        keep(l, n).start()
        act = (jax.nn.silu(g) * u).astype(BF)
        E[s % 2, rows, :] = act
        return rows, act

    def down_grad(k):
        r = dot(ctT[...], E[k % 2], NN).astype(BF).T
        for qq in range(4):
            for t in range(8):
                b_, c_, r_ = down_place(qq, t, k)
                TD[0, b_, c_, r_, :] = r[LN * qq + 16 * t:LN * qq + 16 * (t + 1), :]

    def back_tile(m, s, i, n):
        rows = row_tile(i)
        fetch(n).wait()

        @pl.when(n + 1 < 2 * CH * tiles)
        def _():
            fetch(n + 1).start()

        wgc = columns(m, s)
        wuc = columns(m + 1, s)
        dact = dot(ct[rows, :], down_rows(m + 2, s), NT).astype(BF).astype(F32)
        g = G[n % 2, 0]
        u = G[n % 2, 1]
        sg = jax.nn.sigmoid(g)
        du = (dact * (g * sg)).astype(BF)
        dg = (dact * u * (sg * (1 + g * (1 - sg)))).astype(BF)
        E[0, rows, :] = dg
        E[1, rows, :] = du
        acc[rows, :] += dot(dg, wgc, NT) + dot(du, wuc, NT)

    def back_weights(m, s):
        for j in range(2):
            r = dot(aT[...], E[j], NN).astype(BF)
            for qq in range(4):
                for g in range(8):
                    W[m + j, 2 * g + qq // 2, qq % 2, :, lanes(s)] = r[ROWS * g:ROWS * (g + 1), LN * qq:LN * (qq + 1)]

    def back_norm(out):
        @pl.loop(0, tiles)
        def _(i):
            rows = row_tile(i)
            wide = h[rows, :].astype(F32)
            scale = lax.rsqrt(jnp.mean(wide * wide, -1, keepdims=True) + 1e-6)
            da = acc[rows, :].astype(BF).astype(F32)
            inner = jnp.mean(da * wide, -1, keepdims=True)
            dh = (da * scale - wide * (scale * scale * scale * inner)).astype(BF)
            out[rows, :] = (ct[rows, :].astype(F32) + dh.astype(F32)).astype(BF)

    class Reduce:
        def __init__(self, term, m, n, ln, slot, bufs, ss, rr):
            self.term, self.m, self.n, self.ln = term, m, n, ln
            self.r1, self.r2, self.r3, self.r4, self.s2, self.s3, self.s4 = bufs
            self.slot = slot
            self.c1 = rcopy(term.at[pl.ds(m, n), :, nc, :, ln], self.r1.at[slot], d_core, ss.at[slot, 0], rr.at[slot, 0])
            self.c2 = [rcopy(self.s2[k], self.r2.at[slot, k], (d_y, d_x)[k], ss.at[slot, 1 + k], rr.at[slot, 1 + k]) for k in (0, 1)]
            self.c3 = [rcopy(self.s3[k], self.r3.at[slot, k], (d_x, d_y)[k], ss.at[slot, 3 + k], rr.at[slot, 3 + k]) for k in (0, 1)]
            self.c4 = [rcopy(self.s4[k], self.r4.at[slot, k], d_z[k], ss.at[slot, 5 + k], rr.at[slot, 5 + k]) for k in range(3)]

        def two(self, j, b_):
            return self.term[self.m + j, b_, c, :, self.ln].astype(F32) + self.r1[self.slot, j, b_].astype(F32)

        def send1(self):
            self.c1.start()

        def send2(self):
            self.c1.wait()
            for j in range(self.n):
                for k in range(2):
                    for l in range(2):
                        self.s2[0][j, 2 * k + l] = self.two(j, 8 * k + 4 * ny + l).astype(BF)
                        self.s2[1][j, 2 * k + l] = self.two(j, 8 * nx + 4 * k + 2 + l).astype(BF)
            for cp in self.c2:
                cp.start()

        def send3(self):
            for cp in self.c2:
                cp.wait()
            for j in range(self.n):
                for l in range(2):
                    v = self.two(j, 8 * nx + 4 * y + l) + self.r2[self.slot, 0, j, 2 * nx + l].astype(F32)
                    self.s3[0][j, l] = v.astype(BF)
                    v = self.two(j, 8 * x + 4 * ny + 2 + l) + self.r2[self.slot, 1, j, 2 * ny + l].astype(F32)
                    self.s3[1][j, l] = v.astype(BF)
            for cp in self.c3:
                cp.start()

        def four(self, j, z_):
            h_ = z_ // 2
            l_ = z_ % 2
            v = self.two(j, 8 * x + 4 * y + z_)
            v += self.r2[self.slot, h_, j, 2 * (x * (1 - h_) + y * h_) + l_].astype(F32)
            return v + self.r3[self.slot, h_, j, l_].astype(F32)

        def send4(self):
            for cp in self.c3:
                cp.wait()
            for j in range(self.n):
                for k in range(3):
                    self.s4[k][j] = self.four(j, zs[k]).astype(BF)
            for cp in self.c4:
                cp.start()

        def finish(self, store):
            for cp in self.c4:
                cp.wait()
            for j in range(self.n):
                v = self.four(j, z)
                for k in range(3):
                    v += self.r4[self.slot, k, j].astype(F32)
                store(j, v.astype(BF))

    gu_bufs = (R1, R2, R3, R4, [S2.at[k] for k in range(2)], [S3.at[k] for k in range(2)], [S4.at[k] for k in range(3)])
    d_bufs = (R1d, R2d, R3d, R4d, [TD.at[pl.ds(0, 1), pl.ds(4 * k, 4), nc] for k in range(2)],
              [TD.at[pl.ds(0, 1), pl.ds(8 + 2 * k, 2), nc] for k in range(2)], [TD.at[pl.ds(0, 1), 12 + k, nc] for k in range(3)])

    def layer_of(t):
        return 1 - t // CH

    def gu(t):
        return Reduce(W, 3 * layer_of(t), 2, lanes(t % CH), t % SLOTS, gu_bufs, rs_s, rs_r)

    down = Reduce(TD, 0, 1, pl.ds(0, D), 0, d_bufs, rd_s, rd_r)

    def store_gu(t):
        l = layer_of(t)

        def f(j, v):
            OB[l, j, :, lanes(t % CH)] = v
        return f

    def store_d(t):
        l = 1 - t // CH

        def f(j, v):
            out_d[l] = v
        return f

    def chunk(t, f):
        @pl.when((t >= 0) & (t < 2 * CH))
        def _():
            f(gu(t))

    def yc(l):
        return [rcopy(XS.at[qs[k], pl.ds(2 * l, 2)], XR.at[q, pl.ds(2 * l, 2)], d_q[k], ys_s.at[l, k], ys_r.at[l, k]) for k in range(3)]

    def hand_back(l):
        for j in range(2):
            r = dot(place, OB[l, j], NN).astype(BF)
            for qq in range(GROUP):
                XS[qq, 2 * l + j] = r[PAD * qq:PAD * (qq + 1), :]
        for cp in yc(l):
            cp.start()

    def take_back(l):
        XR[q, pl.ds(2 * l, 2)] = XS[q, pl.ds(2 * l, 2)]
        for cp in yc(l):
            cp.wait()
        for j, o in enumerate((out_g, out_u)):
            for qq in range(GROUP):
                o[l, :, D * qq:D * (qq + 1)] = XR[qq, 2 * l + j, 0:PIECE, :]

    tick(0)
    tick(1)
    loads[2].wait()
    norm_all(True, False)
    tick(2)
    tick(3)
    tick(4)
    tick(5)

    def at(n, k, f):
        @pl.when(n == k)
        def _():
            f()

    def forward_hooks(n):
        def f4():
            st_xy(6)
            st_yx(5)

        def f8():
            st_c(4)
            st_done(3)

        def f12():
            st_xy(7)
            st_yx(6)

        def f16():
            st_c(5)
            st_done(4)

        def f18():
            st_xy(8)
            st_yx(7)

        for k, f in ((4, f4), (8, f8), (12, f12), (16, f16), (18, f18)):
            at(n, k, f)

    @pl.loop(0, CH * tiles)
    def _(n):
        forward_hooks(n)
        s = n // tiles
        i = n % tiles

        @pl.when((i == 0) & (s >= 2))
        def _():
            keep_act(s - 2).wait()

        rows, act = forward_tile(0, s, i, n)

        @pl.when(i == tiles - 1)
        def _():
            keep_act(s).start()

        acc[rows, :] += dot(act, down_rows(2, s), NN)

    @pl.loop(0, tiles)
    def _(i):
        rows = row_tile(i)
        h[rows, :] = (h[rows, :].astype(F32) + acc[rows, :].astype(BF).astype(F32)).astype(BF)

    st_c(6)
    loads[3].wait()
    norm_all(True, True)
    for n in (CH * tiles - 2, CH * tiles - 1):
        keep(0, n).wait()
    for s in (CH - 2, CH - 1):
        keep_act(s).wait()
    st_done(5)

    @pl.loop(0, CH)
    def _(s):
        def f1():
            st_xy(9)
            st_yx(8)
            st_c(7)

        def f2():
            st_done(6)

        def f3():
            st_yx(9)
            st_c(8)

        def f4():
            st_done(7)

        for k, f in ((1, f1), (2, f2), (3, f3), (4, f4)):
            at(s, k, f)

        @pl.loop(0, tiles)
        def _(i):
            forward_tile(1, s, i, s * tiles + i)

        down_grad(s)

    down.send1()
    for n in (CH * tiles - 2, CH * tiles - 1):
        keep(1, n).wait()
    fetch(0).start()
    st_c(9)
    st_done(8)
    st_done(9)

    @pl.loop(0, 2 * CH + 2)
    def _(t):
        m = 3 * (1 - t // CH)
        s = t % CH
        compute = t < 2 * CH

        @pl.when(compute)
        def _():
            @pl.loop(0, tiles)
            def _(i):
                at(i, 2, lambda: chunk(t - 1, lambda r: r.send2()))
                at(i, 3, lambda: chunk(t - 2, lambda r: r.send4()))
                back_tile(m, s, i, t * tiles + i)

            at(s, 0, lambda: down.send2())
            at(s, 1, lambda: down.send3())
            at(s, 2, lambda: down.send4())
            at(s, 3, lambda: down.finish(store_d(t)))
            back_weights(m, s)

        @pl.when(t >= 2 * CH)
        def _():
            chunk(t - 1, lambda r: r.send2())
            chunk(t - 2, lambda r: r.send4())

        chunk(t, lambda r: r.send1())
        chunk(t - 1, lambda r: r.send3())
        chunk(t - 2, lambda r: r.finish(store_gu(t - 2)))

        @pl.when(t == CH - 1)
        def _():
            back_norm(ct)
            again = pltpu.make_async_copy(x_hbm, h, lsem.at[2])
            again.start()
            fetch_act(0).start()
            fetch_act(1).start()
            again.wait()
            norm_all(False, True)

            @pl.loop(0, CH)
            def _(k):
                fetch_act(k).wait()
                down_grad(k)

                @pl.when(k + 2 < CH)
                def _():
                    fetch_act(k + 2).start()

            down.send1()

        @pl.when(t == CH + 1)
        def _():
            hand_back(1)

        @pl.when(t == 2 * CH - 1)
        def _():
            back_norm(ct)
            pltpu.make_async_copy(ct, out_x, lsem.at[3]).start()

    hand_back(0)
    take_back(1)
    take_back(0)
    pltpu.make_async_copy(ct, out_x, lsem.at[3]).wait()


def step(x, dy, wg, wu, wd):
    t = x.shape[1]
    mt = t // TILES
    ag = 16 * 10
    dma = pltpu.SemaphoreType.DMA

    def v(*shape, dtype=BF):
        return pltpu.VMEM(shape, dtype)

    def rs_bufs(slots, n, w):
        r = [v(slots, n, 16, ROWS, w), v(slots, 2, n, 4, ROWS, w), v(slots, 2, n, 2, ROWS, w), v(slots, 3, n, ROWS, w)]
        return r, [v(2, n, 4, ROWS, w), v(2, n, 2, ROWS, w), v(3, n, ROWS, w)]

    gr, gs = rs_bufs(SLOTS, 2, LN)
    dr, _ = rs_bufs(1, 1, D)
    vm = pl.BlockSpec(memory_space=pltpu.VMEM)
    hbm = pl.BlockSpec(memory_space=pl.ANY)
    flops = 17 * 2 * t * D * FF

    def out(*shape, dtype=BF):
        return jax.ShapeDtypeStruct(shape, dtype)

    out_x, out_g, out_u, out_d, _, _ = pl.pallas_call(
        kernel,
        out_shape=(out(t, D), out(LAYERS, PIECE, FF), out(LAYERS, PIECE, FF), out(LAYERS, ROWS, D),
                   out(LAYERS, CH * TILES, 2, mt, FC, dtype=F32), out(CH, t, FC)),
        in_specs=[vm, vm, hbm, hbm, hbm],
        out_specs=(hbm, vm, vm, vm, hbm, hbm),
        scratch_shapes=[
            v(6, 16, 2, ROWS, D), v(t, D), v(t, D), v(t, D), v(D, t), v(D, t), v(t, D, dtype=F32), v(2, t, FC),
            v(2, 2, mt, FC, dtype=F32), v(1, 16, 2, ROWS, D),
            *gr, *gs, *dr,
            v(GROUP, 4, PAD, D), v(GROUP, 4, PAD, D), v(LAYERS, 2, ROWS, D),
            dma((4,)), dma((2,)), dma((2,)), dma((ag,)), dma((ag,)), dma((SLOTS, 8)), dma((SLOTS, 8)), dma((1, 8)), dma((1, 8)),
            dma((3,)), dma((3,)), dma((LAYERS, 3)), dma((LAYERS, 3)),
        ],
        compiler_params=pltpu.CompilerParams(collective_id=0, has_side_effects=True, vmem_limit_bytes=67043328),
        cost_estimate=pl.CostEstimate(flops=flops, bytes_accessed=180_000_000, transcendentals=0),
        name="stack",
    )(wg, wu, wd, x[0], dy[0])
    return out_x[None], out_g, out_u, out_d


def solution(mesh):
    w = P(None, "dp", None)
    t = P(("rep", "dp"), None, None)
    o = P("rep", "dp", None)
    return jax.shard_map(step, mesh=mesh, in_specs=(t, t, w, w, w), out_specs=(t, o, o, o), check_vma=False)
```

time: 350 us -> 304 us (0.87)
  Pallas kernels: 315 us -> 291 us
  blocking collectives: 11.7 us -> 0 us
  waiting for transfers between devices: 7.37 us -> 0 us
  starting transfers between devices: 3.5 us -> 0 us
    pallas_call x1, Pallas kernels: 315 us -> 291 us  [step(): pl.pallas_call(kernel, out_shape=(out(t, D), out(LAYERS, PIECE, FF), out(...]
    all_to_all x1 -> x0, blocking collectives: 11.7 us -> none  [exchange(): return lax.all_to_all(t, 'dp', 0, 0, axis_index_groups=groups, tiled=True)]
    unnamed x16 -> x8, local copies, waits for them, and re-layouts: 3.37 us -> 11.1 us
    all_to_all x1 -> x0, waiting for transfers between devices: 7.37 us -> none  [exchange(): return lax.all_to_all(t, 'dp', 0, 0, axis_index_groups=groups, tiled=True)]
    slice x7 -> x0, local copies, waits for them, and re-layouts: 3.69 us -> none  [the longest x5 2.05 us: step(): wblk = jnp.stack([mine[0], mine[2], wd[0], mine[1], mine[3], wd[1]])]
  transfers between devices with their start and end apart: 1 -> 0, of which waited for: 1 -> 0; matrix products, arithmetic and copies ran while one was open for 0% -> 0% of each run, Pallas kernels for 0% -> 0%
where the time goes in v3:
time: 304 us; the launch traced here: 302 us
  Pallas kernels  291 us (96%)
  local copies, waits for them, and re-layouts  11.1 us (4%)
    pallas_call x1, Pallas kernels, step(): pl.pallas_call(kernel, out_shape=(out(t, D), out(LAYERS, PIECE, FF), out(...  291 us
    unnamed x8, local copies, waits for them, and re-layouts  11.1 us

profile of v3, /device:TPU:0, one launch (start us, length us, event | category | flops | bytes accessed | tf_op | source)
XLA Modules:
  0.0 302.4 jit_solution(11268881981486834372)
XLA Ops:
  0.6 1.6 copy.9.wg
  2.3 1.7 copy.10.wu
  3.9 290.7 %stack.1 = (bf16[2048,640]{1,0:T(8,128)(2,1)}, bf16[2,20,2560]{2,1,0:T(8,128)(2,1)}, bf16[2,20,2560]{2,1,0:T(8,128)(2,1)}, bf16[2,80,640]{2,1,0:T(8,128)(2,1)}, ...) custom-call(bf16[2,20,2560]{2,1,0:T(8,128)(2,1)} %copy.9.wg, bf16[2,20,2560]{2,1,0:T(8,128)(2,1)} %copy.10.wu, ...), custom_call_target="tpu_custom_call" | custom-call | flops 114085068800 | bytes 180000000 | tf_op jit(solution)/shard_map/stack/pallas_call | solution.py:591
  294.6 1.8 copy.11
  296.4 1.8 copy.12
  298.2 0.0 copy-start
  298.2 3.5 %copy.15 = bf16[1,2048,640]{2,1,0:T(8,128)(2,1)} copy(bf16[1,2048,640]{2,1,0:T(8,128)(2,1)} %bitcast.3) | data formatting | bytes 5242880
  301.7 0.0 copy-done
  301.7 0.7 copy.16
Async XLA Ops:
  298.2 3.5 %copy-start = (bf16[2,80,640]{2,1,0:T(8,128)(2,1)S(1)}, bf16[2,80,640]{2,1,0:T(8,128)(2,1)}, u32[]{:S(2)}) copy-start(bf16[2,80,640]{2,1,0:T(8,128)(2,1)} %get-tuple-element.23) | copy-start | bytes 614404

commit v4 on v3

--- a/solution.py
+++ b/solution.py
@@ -77,14 +77,15 @@
                 XS[qq, 2 * l + j] = jnp.zeros((PAD, D), BF)
                 XS[qq, 2 * l + j, 0:PIECE, :] = w[l, :, D * qq:D * (qq + 1)]
 
+    loads[0].wait()
+    loads[1].wait()
     barrier = pltpu.get_barrier_semaphore()
     for d in everyone:
         pl.semaphore_signal(barrier, inc=1, device_id=d, device_id_type=pl.DeviceIdType.MESH)
     pl.semaphore_wait(barrier, len(everyone))
 
-    xc = [rcopy(XS.at[qs[k]], XR.at[q], d_q[k], xs_s.at[k], xs_r.at[k]) for k in range(3)]
-    for cp in xc:
-        cp.start()
+    xc = [[rcopy(XS.at[qs[k], pl.ds(2 * l, 2)], XR.at[q, pl.ds(2 * l, 2)], d_q[k], xs_s.at[l, k], xs_r.at[l, k]) for k in range(3)]
+          for l in range(LAYERS)]
     row = lax.broadcasted_iota(jnp.int32, (ROWS, GROUP * PAD), 0)
     col = lax.broadcasted_iota(jnp.int32, (ROWS, GROUP * PAD), 1)
     inside = col % PAD
@@ -157,28 +158,39 @@
         if 0 <= k - 3 < len(msgs):
             st_done(k - 3)
 
-    loads[0].wait()
-    loads[1].wait()
-    st_z(0)
-    st_z(1)
-    XR[q] = XS[q]
-    for cp in xc:
-        cp.wait()
-    for l in range(LAYERS):
+    def own_blocks(l):
+        for cp in xc[l]:
+            cp.wait()
         for j in range(2):
             pieces = XR[:, 2 * l + j].reshape(GROUP * PAD, D)
             W[3 * l + j, b, c] = dot(pick, pieces, NN).astype(BF)
-    for i in range(2, len(msgs)):
+
+    st_z(0)
+    start(xc[0])
+    st_z(1)
+    XR[q] = XS[q]
+    own_blocks(0)
+    for i in (2, 3, 4):
         st_z(i)
+    start(xc[1])
+
+    def sigmoid(t):
+        return 0.5 * jnp.tanh(0.5 * t) + 0.5
+
+    halves = 2
+    ht = mt // halves
+
+    def sub_tile(i, k):
+        return pl.ds(aligned(i * mt + k * ht, ht), ht)
 
     def row_tile(i):
         return pl.ds(aligned(i * mt, mt), mt)
 
-    def norm_all(with_a, with_t):
+    def norm_all(src, with_a, with_t):
         @pl.loop(0, tiles)
         def _(i):
             rows = row_tile(i)
-            wide = h[rows, :].astype(F32)
+            wide = src[rows, :].astype(F32)
             scale = lax.rsqrt(jnp.mean(wide * wide, -1, keepdims=True) + 1e-6)
             v = (wide * scale).astype(BF)
             if with_a:
@@ -197,24 +209,24 @@
             cols.append(jnp.concatenate([W[m, 2 * g + q // 2, q % 2, :, lanes(s)] for g in range(8)], axis=0))
         return jnp.concatenate(cols, axis=1)
 
-    def down_place(q, t, s):
-        j = 8 * s + t
-        k = 8 * q + j // 5
-        return k // 2, k % 2, pl.ds(aligned((j % 5) * 16, 16), 16)
+    def down_places(s):
+        at_t = []
+        for t in range(8):
+            j = 8 * s + t
+            k = lax.div(j, 5)
+            at_t.append((lax.div(k, 2), lax.rem(k, 2), pl.ds(pl.multiple_of(lax.rem(j, 5) * 16, 16), 16)))
+        return [[(4 * q_ + b_, c_, r_) for b_, c_, r_ in at_t] for q_ in range(4)]
 
     def down_rows(m, s):
-        rows = []
-        for q in range(4):
-            for t in range(8):
-                b_, c_, r_ = down_place(q, t, s)
-                rows.append(W[m, b_, c_, r_, :])
-        return jnp.concatenate(rows, axis=0)
+        return jnp.concatenate([W[m, b_, c_, r_, :] for by_t in down_places(s) for b_, c_, r_ in by_t], axis=0)
 
     def keep(l, n):
         return pltpu.make_async_copy(G.at[n % 2], gu_hbm.at[l, n], gsem.at[n % 2])
 
     def fetch(n):
-        return pltpu.make_async_copy(gu_hbm.at[1 - n // (CH * tiles), n % (CH * tiles)], G.at[n % 2], gsem.at[n % 2])
+        if isinstance(n, int):
+            return pltpu.make_async_copy(gu_hbm.at[1 - n // (CH * tiles), n % (CH * tiles)], G.at[n % 2], gsem.at[n % 2])
+        return pltpu.make_async_copy(gu_hbm.at[1 - lax.div(n, CH * tiles), lax.rem(n, CH * tiles)], G.at[lax.rem(n, 2)], gsem.at[lax.rem(n, 2)])
 
     def keep_act(s):
         return pltpu.make_async_copy(E.at[s % 2], act_hbm.at[s], esem.at[s % 2])
@@ -223,31 +235,32 @@
         return pltpu.make_async_copy(act_hbm.at[s], E.at[s % 2], esem.at[s % 2])
 
     def forward_tile(l, s, i, n):
-        rows = row_tile(i)
-
         @pl.when(n >= 2)
         def _():
             keep(l, n - 2).wait()
 
-        v = a[rows, :]
-        g = dot(v, columns(3 * l, s), NN)
-        u = dot(v, columns(3 * l + 1, s), NN)
-        G[n % 2, 0] = g
-        G[n % 2, 1] = u
+        wgc = columns(3 * l, s)
+        wuc = columns(3 * l + 1, s)
+        gu_ = []
+        for k in range(halves):
+            v = a[sub_tile(i, k), :]
+            gu_.append((dot(v, wgc, NN), dot(v, wuc, NN)))
+        for k, (g, u) in enumerate(gu_):
+            G[lax.rem(n, 2), 0, k * ht:(k + 1) * ht, :] = g
+            G[lax.rem(n, 2), 1, k * ht:(k + 1) * ht, :] = u
+            act = (g * sigmoid(g) * u).astype(BF)
+            E[s % 2, sub_tile(i, k), :] = act
+            if l == 0:
+                acc[sub_tile(i, k), :] += dot(act, down_rows(2, s), NN)
         keep(l, n).start()
-        act = (jax.nn.silu(g) * u).astype(BF)
-        E[s % 2, rows, :] = act
-        return rows, act
 
     def down_grad(k):
         r = dot(ctT[...], E[k % 2], NN).astype(BF).T
-        for qq in range(4):
-            for t in range(8):
-                b_, c_, r_ = down_place(qq, t, k)
+        for qq, by_t in enumerate(down_places(k)):
+            for t, (b_, c_, r_) in enumerate(by_t):
                 TD[0, b_, c_, r_, :] = r[LN * qq + 16 * t:LN * qq + 16 * (t + 1), :]
 
     def back_tile(m, s, i, n):
-        rows = row_tile(i)
         fetch(n).wait()
 
         @pl.when(n + 1 < 2 * CH * tiles)
@@ -256,15 +269,20 @@
 
         wgc = columns(m, s)
         wuc = columns(m + 1, s)
-        dact = dot(ct[rows, :], down_rows(m + 2, s), NT).astype(BF).astype(F32)
-        g = G[n % 2, 0]
-        u = G[n % 2, 1]
-        sg = jax.nn.sigmoid(g)
-        du = (dact * (g * sg)).astype(BF)
-        dg = (dact * u * (sg * (1 + g * (1 - sg)))).astype(BF)
-        E[0, rows, :] = dg
-        E[1, rows, :] = du
-        acc[rows, :] += dot(dg, wgc, NT) + dot(du, wuc, NT)
+        wdr = down_rows(m + 2, s)
+        both = jnp.concatenate([wgc, wuc], axis=1)
+        dacts = [dot(ct[sub_tile(i, k), :], wdr, NT) for k in range(halves)]
+        for k in range(halves):
+            dact = dacts[k].astype(BF).astype(F32)
+            g = G[lax.rem(n, 2), 0, k * ht:(k + 1) * ht, :]
+            u = G[lax.rem(n, 2), 1, k * ht:(k + 1) * ht, :]
+            sg = sigmoid(g)
+            si = g * sg
+            du = (dact * si).astype(BF)
+            dg = (dact * u * (sg + si * (1 - sg))).astype(BF)
+            E[0, sub_tile(i, k), :] = dg
+            E[1, sub_tile(i, k), :] = du
+            acc[sub_tile(i, k), :] += dot(jnp.concatenate([dg, du], axis=1), both, NT)
 
     def back_weights(m, s):
         for j in range(2):
@@ -273,16 +291,16 @@
                 for g in range(8):
                     W[m + j, 2 * g + qq // 2, qq % 2, :, lanes(s)] = r[ROWS * g:ROWS * (g + 1), LN * qq:LN * (qq + 1)]
 
-    def back_norm(out):
+    def back_norm(src):
         @pl.loop(0, tiles)
         def _(i):
             rows = row_tile(i)
-            wide = h[rows, :].astype(F32)
+            wide = src[rows, :].astype(F32)
             scale = lax.rsqrt(jnp.mean(wide * wide, -1, keepdims=True) + 1e-6)
             da = acc[rows, :].astype(BF).astype(F32)
             inner = jnp.mean(da * wide, -1, keepdims=True)
             dh = (da * scale - wide * (scale * scale * scale * inner)).astype(BF)
-            out[rows, :] = (ct[rows, :].astype(F32) + dh.astype(F32)).astype(BF)
+            ct[rows, :] = (ct[rows, :].astype(F32) + dh.astype(F32)).astype(BF)
 
     class Reduce:
         def __init__(self, term, m, n, ln, slot, bufs, ss, rr):
@@ -352,10 +370,10 @@
               [TD.at[pl.ds(0, 1), pl.ds(8 + 2 * k, 2), nc] for k in range(2)], [TD.at[pl.ds(0, 1), 12 + k, nc] for k in range(3)])
 
     def layer_of(t):
-        return 1 - t // CH
+        return 1 - lax.div(t, CH)
 
     def gu(t):
-        return Reduce(W, 3 * layer_of(t), 2, lanes(t % CH), t % SLOTS, gu_bufs, rs_s, rs_r)
+        return Reduce(W, 3 * layer_of(t), 2, lanes(lax.rem(t, CH)), lax.rem(t, SLOTS), gu_bufs, rs_s, rs_r)
 
     down = Reduce(TD, 0, 1, pl.ds(0, D), 0, d_bufs, rd_s, rd_r)
 
@@ -363,11 +381,11 @@
         l = layer_of(t)
 
         def f(j, v):
-            OB[l, j, :, lanes(t % CH)] = v
+            OB[l, j, :, lanes(lax.rem(t, CH))] = v
         return f
 
     def store_d(t):
-        l = 1 - t // CH
+        l = layer_of(t)
 
         def f(j, v):
             out_d[l] = v
@@ -399,8 +417,11 @@
 
     tick(0)
     tick(1)
+    own_blocks(1)
+    for i in range(5, len(msgs)):
+        st_z(i)
     loads[2].wait()
-    norm_all(True, False)
+    norm_all(h, True, False)
     tick(2)
     tick(3)
     tick(4)
@@ -438,20 +459,18 @@
     @pl.loop(0, CH * tiles)
     def _(n):
         forward_hooks(n)
-        s = n // tiles
-        i = n % tiles
+        s = lax.div(n, tiles)
+        i = lax.rem(n, tiles)
 
         @pl.when((i == 0) & (s >= 2))
         def _():
             keep_act(s - 2).wait()
 
-        rows, act = forward_tile(0, s, i, n)
+        forward_tile(0, s, i, n)
 
         @pl.when(i == tiles - 1)
         def _():
             keep_act(s).start()
-
-        acc[rows, :] += dot(act, down_rows(2, s), NN)
 
     @pl.loop(0, tiles)
     def _(i):
@@ -460,7 +479,7 @@
 
     st_c(6)
     loads[3].wait()
-    norm_all(True, True)
+    norm_all(h, True, True)
     for n in (CH * tiles - 2, CH * tiles - 1):
         keep(0, n).wait()
     for s in (CH - 2, CH - 1):
@@ -497,14 +516,15 @@
     for n in (CH * tiles - 2, CH * tiles - 1):
         keep(1, n).wait()
     fetch(0).start()
+    pltpu.make_async_copy(x_hbm, a, lsem.at[2]).start()
     st_c(9)
     st_done(8)
     st_done(9)
 
     @pl.loop(0, 2 * CH + 2)
     def _(t):
-        m = 3 * (1 - t // CH)
-        s = t % CH
+        m = 3 * (1 - lax.div(t, CH))
+        s = lax.rem(t, CH)
         compute = t < 2 * CH
 
         @pl.when(compute)
@@ -532,13 +552,11 @@
 
         @pl.when(t == CH - 1)
         def _():
-            back_norm(ct)
-            again = pltpu.make_async_copy(x_hbm, h, lsem.at[2])
-            again.start()
             fetch_act(0).start()
             fetch_act(1).start()
-            again.wait()
-            norm_all(False, True)
+            back_norm(h)
+            pltpu.make_async_copy(x_hbm, a, lsem.at[2]).wait()
+            norm_all(a, False, True)
 
             @pl.loop(0, CH)
             def _(k):
@@ -557,7 +575,7 @@
 
         @pl.when(t == 2 * CH - 1)
         def _():
-            back_norm(ct)
+            back_norm(a)
             pltpu.make_async_copy(ct, out_x, lsem.at[3]).start()
 
     hand_back(0)
@@ -600,7 +618,7 @@
             *gr, *gs, *dr,
             v(GROUP, 4, PAD, D), v(GROUP, 4, PAD, D), v(LAYERS, 2, ROWS, D),
             dma((4,)), dma((2,)), dma((2,)), dma((ag,)), dma((ag,)), dma((SLOTS, 8)), dma((SLOTS, 8)), dma((1, 8)), dma((1, 8)),
-            dma((3,)), dma((3,)), dma((LAYERS, 3)), dma((LAYERS, 3)),
+            dma((LAYERS, 3)), dma((LAYERS, 3)), dma((LAYERS, 3)), dma((LAYERS, 3)),
         ],
         compiler_params=pltpu.CompilerParams(collective_id=0, has_side_effects=True, vmem_limit_bytes=67043328),
         cost_estimate=pl.CostEstimate(flops=flops, bytes_accessed=180_000_000, transcendentals=0),

time: 304 us -> 306 us (level)
  no operation moved by 1% of the time
where the time goes in v4:
time: 306 us; the launch traced here: 305 us
  Pallas kernels  293 us (96%)
  local copies, waits for them, and re-layouts  11.1 us (4%)
    pallas_call x1, Pallas kernels, step(): pl.pallas_call(kernel, out_shape=(out(t, D), out(LAYERS, PIECE, FF), out(...  293 us
    unnamed x8, local copies, waits for them, and re-layouts  11.1 us

profile of v4, /device:TPU:0, one launch (start us, length us, event | category | flops | bytes accessed | tf_op | source)
XLA Modules:
  0.0 304.6 jit_solution(13400244018150892341)
XLA Ops:
  0.6 1.6 copy.9.wg
  2.3 1.7 copy.10.wu
  3.9 292.9 %stack.1 = (bf16[2048,640]{1,0:T(8,128)(2,1)}, bf16[2,20,2560]{2,1,0:T(8,128)(2,1)}, bf16[2,20,2560]{2,1,0:T(8,128)(2,1)}, bf16[2,80,640]{2,1,0:T(8,128)(2,1)}, ...) custom-call(bf16[2,20,2560]{2,1,0:T(8,128)(2,1)} %copy.9.wg, bf16[2,20,2560]{2,1,0:T(8,128)(2,1)} %copy.10.wu, ...), custom_call_target="tpu_custom_call" | custom-call | flops 114085068800 | bytes 180000000 | tf_op jit(solution)/shard_map/stack/pallas_call | solution.py:609
  296.9 1.8 copy.11
  298.7 1.8 copy.12
  300.5 0.0 copy-start
  300.5 3.5 %copy.15 = bf16[1,2048,640]{2,1,0:T(8,128)(2,1)} copy(bf16[1,2048,640]{2,1,0:T(8,128)(2,1)} %bitcast.3) | data formatting | bytes 5242880
  304.0 0.0 copy-done
  304.0 0.7 copy.16
Async XLA Ops:
  300.5 3.5 %copy-start = (bf16[2,80,640]{2,1,0:T(8,128)(2,1)S(1)}, bf16[2,80,640]{2,1,0:T(8,128)(2,1)}, u32[]{:S(2)}) copy-start(bf16[2,80,640]{2,1,0:T(8,128)(2,1)} %get-tuple-element.23) | copy-start | bytes 614404

commit v5 on v4

--- a/solution.py
+++ b/solution.py
@@ -17,6 +17,7 @@
 GROUP = 4
 PIECE = 20
 PAD = 32
+PARTS = 8
 TILES = 4
 SLOTS = 4
 NN = ((1,), (0,))
@@ -66,6 +67,9 @@
         return pltpu.make_async_remote_copy(src_ref=src, dst_ref=dst, send_sem=ss, recv_sem=rr,
                                             device_id=d, device_id_type=pl.DeviceIdType.MESH)
 
+    barrier = pltpu.get_barrier_semaphore()
+    for d in everyone:
+        pl.semaphore_signal(barrier, inc=1, device_id=d, device_id_type=pl.DeviceIdType.MESH)
     loads = [pltpu.make_async_copy(wd_hbm.at[l], W.at[3 * l + 2, b, c], lsem.at[l]) for l in range(LAYERS)]
     loads.append(pltpu.make_async_copy(x_hbm, h, lsem.at[2]))
     loads.append(pltpu.make_async_copy(dy_hbm, ct, lsem.at[3]))
@@ -79,9 +83,6 @@
 
     loads[0].wait()
     loads[1].wait()
-    barrier = pltpu.get_barrier_semaphore()
-    for d in everyone:
-        pl.semaphore_signal(barrier, inc=1, device_id=d, device_id_type=pl.DeviceIdType.MESH)
     pl.semaphore_wait(barrier, len(everyone))
 
     xc = [[rcopy(XS.at[qs[k], pl.ds(2 * l, 2)], XR.at[q, pl.ds(2 * l, 2)], d_q[k], xs_s.at[l, k], xs_r.at[l, k]) for k in range(3)]
@@ -118,9 +119,10 @@
     for g in msgs:
         zc.append([push(g, b, 1, d) for d in d_z])
         xy.append([push(g, base, 2, d_x), push(g, base + 2, 2, d_y)])
-        yx.append([push(g, 4 * y, 2, d_y), push(g, 8 + 4 * y, 2, d_y), push(g, 8 * x + 2, 2, d_x), push(g, 8 * x + 6, 2, d_x)])
-        cc.append([push(g, base, 4, d_core), push(g, 8 * nx + 4 * y, 2, d_core), push(g, 8 * x + 4 * ny + 2, 2, d_core),
-                   push(g, 4 * ny, 2, d_core), push(g, 8 + 4 * ny, 2, d_core), push(g, 8 * nx + 2, 2, d_core), push(g, 8 * nx + 6, 2, d_core)])
+        xs2, ys2 = (lambda y_: (4 * y_, 8 + 4 * y_)), (lambda x_: (8 * x_ + 2, 8 * x_ + 6))
+        yx.append([push(g, f, 2, d_y) for f in xs2(y)] + [push(g, f, 2, d_x) for f in ys2(x)])
+        late = [8 * nx + 4 * y, 8 * x + 4 * ny + 2, *xs2(ny), *ys2(nx)]
+        cc.append([push(g, base, 4, d_core)] + [push(g, f, 2, d_core) for f in late])
 
     def st_z(i):
         start(zc[i])
@@ -220,13 +222,37 @@
     def down_rows(m, s):
         return jnp.concatenate([W[m, b_, c_, r_, :] for by_t in down_places(s) for b_, c_, r_ in by_t], axis=0)
 
+    class Several:
+        def __init__(self, copies):
+            self.copies = copies
+
+        def start(self):
+            for cp in self.copies:
+                cp.start()
+
+        def wait(self):
+            for cp in self.copies:
+                cp.wait()
+
+    def div(i, n):
+        return i // n if isinstance(i, int) else lax.div(i, n)
+
+    def rem(i, n):
+        return i % n if isinstance(i, int) else lax.rem(i, n)
+
+    def pieces_of(l, n, slot, out):
+        copies = []
+        for k in range(PARTS):
+            j, r = k // (PARTS // 2), pl.ds(k % (PARTS // 2) * (mt // (PARTS // 2)), mt // (PARTS // 2))
+            here, there = G.at[slot, j, r], gu_hbm.at[l, n, j, r]
+            copies.append(pltpu.make_async_copy(here, there, gsem.at[slot, k]) if out else pltpu.make_async_copy(there, here, gsem.at[slot, k]))
+        return Several(copies)
+
     def keep(l, n):
-        return pltpu.make_async_copy(G.at[n % 2], gu_hbm.at[l, n], gsem.at[n % 2])
+        return pieces_of(l, n, rem(n, 2), True)
 
     def fetch(n):
-        if isinstance(n, int):
-            return pltpu.make_async_copy(gu_hbm.at[1 - n // (CH * tiles), n % (CH * tiles)], G.at[n % 2], gsem.at[n % 2])
-        return pltpu.make_async_copy(gu_hbm.at[1 - lax.div(n, CH * tiles), lax.rem(n, CH * tiles)], G.at[lax.rem(n, 2)], gsem.at[lax.rem(n, 2)])
+        return pieces_of(1 - div(n, CH * tiles), rem(n, CH * tiles), rem(n, 2), False)
 
     def keep_act(s):
         return pltpu.make_async_copy(E.at[s % 2], act_hbm.at[s], esem.at[s % 2])
@@ -417,15 +443,15 @@
 
     tick(0)
     tick(1)
+    loads[2].wait()
+    norm_all(h, True, False)
+    tick(2)
     own_blocks(1)
     for i in range(5, len(msgs)):
         st_z(i)
-    loads[2].wait()
-    norm_all(h, True, False)
-    tick(2)
     tick(3)
     tick(4)
-    tick(5)
+    st_done(2)
 
     def at(n, k, f):
         @pl.when(n == k)
@@ -433,28 +459,17 @@
             f()
 
     def forward_hooks(n):
-        def f4():
-            st_xy(6)
-            st_yx(5)
-
-        def f8():
-            st_c(4)
-            st_done(3)
-
-        def f12():
-            st_xy(7)
-            st_yx(6)
-
-        def f16():
-            st_c(5)
-            st_done(4)
-
-        def f18():
-            st_xy(8)
-            st_yx(7)
-
-        for k, f in ((4, f4), (8, f8), (12, f12), (16, f16), (18, f18)):
-            at(n, k, f)
+        for k, calls in (
+            (2, ((st_xy, 5), (st_yx, 4))),
+            (5, ((st_c, 3),)),
+            (8, ((st_done, 3), (st_xy, 6), (st_yx, 5))),
+            (11, ((st_c, 4),)),
+            (14, ((st_xy, 7), (st_yx, 6))),
+            (16, ((st_done, 4),)),
+            (17, ((st_c, 5),)),
+            (19, ((st_xy, 8), (st_yx, 7))),
+        ):
+            at(n, k, lambda: [f(i) for f, i in calls] and None)
 
     @pl.loop(0, CH * tiles)
     def _(n):
@@ -488,23 +503,13 @@
 
     @pl.loop(0, CH)
     def _(s):
-        def f1():
-            st_xy(9)
-            st_yx(8)
-            st_c(7)
-
-        def f2():
-            st_done(6)
-
-        def f3():
-            st_yx(9)
-            st_c(8)
-
-        def f4():
-            st_done(7)
-
-        for k, f in ((1, f1), (2, f2), (3, f3), (4, f4)):
-            at(s, k, f)
+        for k, calls in (
+            (1, ((st_xy, 9), (st_yx, 8))),
+            (2, ((st_done, 6), (st_c, 7))),
+            (3, ((st_yx, 9), (st_c, 8))),
+            (4, ((st_done, 7),)),
+        ):
+            at(s, k, lambda: [f(i) for f, i in calls] and None)
 
         @pl.loop(0, tiles)
         def _(i):
@@ -521,7 +526,7 @@
     st_done(8)
     st_done(9)
 
-    @pl.loop(0, 2 * CH + 2)
+    @pl.loop(0, 2 * CH + 3)
     def _(t):
         m = 3 * (1 - lax.div(t, CH))
         s = lax.rem(t, CH)
@@ -531,6 +536,7 @@
         def _():
             @pl.loop(0, tiles)
             def _(i):
+                at(i, 1, lambda: chunk(t - 3, lambda r: r.finish(store_gu(t - 3))))
                 at(i, 2, lambda: chunk(t - 1, lambda r: r.send2()))
                 at(i, 3, lambda: chunk(t - 2, lambda r: r.send4()))
                 back_tile(m, s, i, t * tiles + i)
@@ -544,11 +550,16 @@
         @pl.when(t >= 2 * CH)
         def _():
             chunk(t - 1, lambda r: r.send2())
+            chunk(t - 3, lambda r: r.finish(store_gu(t - 3)))
             chunk(t - 2, lambda r: r.send4())
+
+            @pl.when(t == 2 * CH)
+            def _():
+                back_norm(a)
+                pltpu.make_async_copy(ct, out_x, lsem.at[3]).start()
 
         chunk(t, lambda r: r.send1())
         chunk(t - 1, lambda r: r.send3())
-        chunk(t - 2, lambda r: r.finish(store_gu(t - 2)))
 
         @pl.when(t == CH - 1)
         def _():
@@ -569,17 +580,15 @@
 
             down.send1()
 
-        @pl.when(t == CH + 1)
+        @pl.when(t == CH + 2)
         def _():
             hand_back(1)
 
         @pl.when(t == 2 * CH - 1)
         def _():
-            back_norm(a)
-            pltpu.make_async_copy(ct, out_x, lsem.at[3]).start()
+            take_back(1)
 
     hand_back(0)
-    take_back(1)
     take_back(0)
     pltpu.make_async_copy(ct, out_x, lsem.at[3]).wait()
 
@@ -617,7 +626,7 @@
             v(2, 2, mt, FC, dtype=F32), v(1, 16, 2, ROWS, D),
             *gr, *gs, *dr,
             v(GROUP, 4, PAD, D), v(GROUP, 4, PAD, D), v(LAYERS, 2, ROWS, D),
-            dma((4,)), dma((2,)), dma((2,)), dma((ag,)), dma((ag,)), dma((SLOTS, 8)), dma((SLOTS, 8)), dma((1, 8)), dma((1, 8)),
+            dma((4,)), dma((2, PARTS)), dma((2,)), dma((ag,)), dma((ag,)), dma((SLOTS, 8)), dma((SLOTS, 8)), dma((1, 8)), dma((1, 8)),
             dma((LAYERS, 3)), dma((LAYERS, 3)), dma((LAYERS, 3)), dma((LAYERS, 3)),
         ],
         compiler_params=pltpu.CompilerParams(collective_id=0, has_side_effects=True, vmem_limit_bytes=67043328),

time: 306 us -> 286 us (0.935)
  Pallas kernels: 293 us -> 274 us
    pallas_call x1, Pallas kernels: 293 us -> 274 us  [step(): pl.pallas_call(kernel, out_shape=(out(t, D), out(LAYERS, PIECE, FF), out(...]
where the time goes in v5:
time: 286 us; the launch traced here: 285 us
  Pallas kernels  274 us (96%)
  local copies, waits for them, and re-layouts  11.1 us (4%)
    pallas_call x1, Pallas kernels, step(): pl.pallas_call(kernel, out_shape=(out(t, D), out(LAYERS, PIECE, FF), out(...  274 us
    unnamed x8, local copies, waits for them, and re-layouts  11.1 us

profile of v5, /device:TPU:0, one launch (start us, length us, event | category | flops | bytes accessed | tf_op | source)
XLA Modules:
  0.0 285.5 jit_solution(5248918739176742510)
XLA Ops:
  0.6 1.6 copy.9.wg
  2.3 1.7 copy.10.wu
  3.9 273.8 %stack.1 = (bf16[2048,640]{1,0:T(8,128)(2,1)}, bf16[2,20,2560]{2,1,0:T(8,128)(2,1)}, bf16[2,20,2560]{2,1,0:T(8,128)(2,1)}, bf16[2,80,640]{2,1,0:T(8,128)(2,1)}, ...) custom-call(bf16[2,20,2560]{2,1,0:T(8,128)(2,1)} %copy.9.wg, bf16[2,20,2560]{2,1,0:T(8,128)(2,1)} %copy.10.wu, ...), custom_call_target="tpu_custom_call" | custom-call | flops 114085068800 | bytes 180000000 | tf_op jit(solution)/shard_map/stack/pallas_call | solution.py:618
  277.7 1.8 copy.11
  279.5 1.8 copy.12
  281.3 0.0 copy-start
  281.3 3.5 %copy.15 = bf16[1,2048,640]{2,1,0:T(8,128)(2,1)} copy(bf16[1,2048,640]{2,1,0:T(8,128)(2,1)} %bitcast.3) | data formatting | bytes 5242880
  284.8 0.0 copy-done
  284.8 0.7 copy.16
Async XLA Ops:
  281.3 3.5 %copy-start = (bf16[2,80,640]{2,1,0:T(8,128)(2,1)S(1)}, bf16[2,80,640]{2,1,0:T(8,128)(2,1)}, u32[]{:S(2)}) copy-start(bf16[2,80,640]{2,1,0:T(8,128)(2,1)} %get-tuple-element.23) | copy-start | bytes 614404
